TPU v7x, 512 devices: a whole 4x8x8 slice. The times are simulated.
512 devices in a mesh: sub: 32 (over x_lo, y, core), dir: 16 (over x_hi, z).
Axes of the slice: x: 4 (x_hi: 2, x_lo: 2; x = x_hi * 2 + x_lo), y: 8, z: 8, core: 2. Of those that a mesh axis runs over, the one named last changes fastest.
Arguments:
- fine_fields: float32 [32768, 2, 1024], P(('sub', 'dir')), may hold values from -6 to 6
- fine_octant: int32 [32768], P(('sub', 'dir')), may hold values from 0 to 7, as said below
- mid_octant: int32 [4096], P('sub'), may hold values from 0 to 7, as said below
- shift_fine: float32 [8, 4096], replicated, may hold values from -3.140625 to 3.140625
- shift_mid: float32 [8, 16384], replicated, may hold values from -3.140625 to 3.140625
- interp_theta_mid: float32 [64, 32], replicated, may hold values from -1 to 1
- interp_phi_mid: float32 [64, 32], replicated, may hold values from -1 to 1
- interp_theta_top: float32 [128, 64], replicated, may hold values from -0.75 to 0.75
- interp_phi_top: float32 [128, 64], replicated, may hold values from -0.75 to 0.75
- partners: int32 [512, 32], P('sub'), may hold values from 0 to 511, as said below
- translation: float32 [512, 32, 2, 16384], P('sub', None, None, 'dir'), may hold values from -0.0234375 to 0.0234375
Outputs:
- fine_incoming: float32 [32768, 2, 1024], P(('sub', 'dir'))
Inputs may be any that keep to these rules, and one draw needn't show every extreme that they name: `fine_octant`: each aligned group of 8 entries is a permutation of 0 to 7. `mid_octant`: each aligned group of 8 entries is a permutation of 0 to 7. `partners`: row t names 32 different top boxes, none of them t.
All inputs are finite; a program needn't handle non-finite values.
Results may differ from a plain program's by a relative error of at most 0.000096.
Values sent between devices are 32-bit elements; how exact they have to be, the bound alone decides.
No kernel may reach another device: no remote copies, remote signals or barrier semaphores. Data moves between devices by JAX's collectives and lax.ppermute only.
A program may use at most 64 MiB of HBM per device.

v0:
```python
import jax
import jax.numpy as jnp
from jax import lax
from jax.experimental import pallas as pl
from jax.experimental.pallas import tpu as pltpu
from jax.sharding import PartitionSpec as P


F32 = jnp.float32
BF16 = jnp.bfloat16
VMEM = pl.BlockSpec(memory_space=pltpu.VMEM)
SMEM = pl.BlockSpec(memory_space=pltpu.SMEM)
UP_GROUP, TOP_GROUP, DOWN_GROUP = 4, 2, 4
ANY = pl.BlockSpec(memory_space=pl.ANY)


def split(x):
    high = x.astype(BF16)
    return high, (x - high.astype(F32)).astype(BF16)


def dot(a, b, dims=((1,), (0,))):
    return lax.dot_general(a, b, (dims, ((), ())), preferred_element_type=F32)


def onehot(shape, source):
    rows = lax.broadcasted_iota(jnp.int32, shape, 0)
    cols = lax.broadcasted_iota(jnp.int32, shape, 1)
    return jnp.where(source(rows, cols), 1.0, 0.0).astype(BF16)


def cos_sin(angles):
    half = angles * 0.5
    square = half * half
    sine = -1.0 / 39916800.0
    for term in (1.0 / 362880.0, -1.0 / 5040.0, 1.0 / 120.0, -1.0 / 6.0, 1.0):
        sine = sine * square + term
    sine = sine * half
    cosine = 1.0 / 479001600.0
    for term in (-1.0 / 3628800.0, 1.0 / 40320.0, -1.0 / 720.0, 1.0 / 24.0, -0.5, 1.0):
        cosine = cosine * square + term
    return 1.0 - 2.0 * (sine * sine), 2.0 * (sine * cosine)


def group_transpose(v):
    lane = lax.broadcasted_iota(jnp.int32, v[0].shape, 1)
    low = lane < 64
    even = (lane // 32) % 2 == 0
    roll = lambda x, by: pltpu.roll(x, by, 1)
    x0 = jnp.where(low, v[0], roll(v[2], 64))
    x2 = jnp.where(low, roll(v[0], 64), v[2])
    x1 = jnp.where(low, v[1], roll(v[3], 64))
    x3 = jnp.where(low, roll(v[1], 64), v[3])
    return [
        jnp.where(even, x0, roll(x1, 32)),
        jnp.where(even, roll(x0, 96), x1),
        jnp.where(even, x2, roll(x3, 32)),
        jnp.where(even, roll(x2, 96), x3),
    ]


def invert(octants, inverse, count, first):
    def step(i, _):
        inverse[(i // 8) * 8 + octants[first + i]] = i
        return 0

    lax.fori_loop(0, count, step, 0, unroll=8)


def fine_tables(angle_ref, cos_ref, sin_ref):
    for pair in range(4):
        first = angle_ref[pl.ds(2 * pair, 32, stride=8), :]
        second = angle_ref[pl.ds(2 * pair + 1, 32, stride=8), :]
        low = lax.broadcasted_iota(jnp.int32, first.shape, 1) < 64
        for odd, angles in enumerate(
            (
                jnp.where(low, first, pltpu.roll(second, 64, 1)),
                jnp.where(low, pltpu.roll(first, 64, 1), second),
            )
        ):
            cosine, sine = cos_sin(angles)
            cos_ref[pair, pl.ds(32 * odd, 32), :] = cosine
            sin_ref[pair, pl.ds(32 * odd, 32), :] = sine


def top_tables(angle_ref, cos_ref, sin_ref):
    for i in range(16):
        cosine, sine = cos_sin(angle_ref[pl.ds(64 * i, 64), :])
        cos_ref[pl.ds(64 * i, 64), :] = cosine
        sin_ref[pl.ds(64 * i, 64), :] = sine


def block_diagonal(matrix, copies):
    n, k = matrix.shape
    spread = onehot((k, copies * k), lambda r, c: c % k == r)
    out = []
    for part in split(matrix):
        wide = dot(part, spread)
        tall = jnp.concatenate([wide] * copies, axis=0)
        rows = lax.broadcasted_iota(jnp.int32, tall.shape, 0) // n
        cols = lax.broadcasted_iota(jnp.int32, tall.shape, 1) // k
        out.append(jnp.where(rows == cols, tall, 0.0).astype(BF16))
    return out


def theta_up(theta, rows, cols):
    targets, sources = theta.shape[1], theta.shape[0]
    high, low = [
        dot(onehot((targets, targets), rows), part, ((1,), (1,))).astype(BF16)
        for part in split(theta)
    ]
    wide = (sources, 3 * sources)
    order = lambda r, c: cols(r, c % sources)
    first = onehot(wide, lambda r, c: order(r, c) & (c < 2 * sources))
    last = onehot(wide, lambda r, c: order(r, c) & (c >= 2 * sources))
    return (dot(high, first) + dot(low, last)).astype(BF16)


def theta_down(theta, rows, cols):
    sources, targets = theta.shape
    high, low = [
        dot(onehot((sources, sources), rows), part).astype(BF16) for part in split(theta)
    ]
    wide = (targets, 3 * targets)
    order = lambda r, c: cols(r, c % targets)
    first = onehot(wide, lambda r, c: order(r, c) & (c < 2 * targets))
    last = onehot(wide, lambda r, c: order(r, c) & (c >= 2 * targets))
    return (dot(high, first) + dot(low, last)).astype(BF16)


def up_kernel(
    fine_hbm, fine_oct, mid_oct, angle_fine_hbm, angle_mid_hbm,
    theta_mid, phi_mid, theta_top, phi_top,
    out, fine_inv, mid_inv, cos_f, sin_f, cos_t, sin_t, mids,
    fine, angle_fine, angle_mid, sems,
):
    loads = [
        pltpu.make_async_copy(source, target, sems.at[i])
        for i, (source, target) in enumerate(
            ((angle_fine_hbm, angle_fine), (fine_hbm, fine), (angle_mid_hbm, angle_mid))
        )
    ]
    for load in loads:
        load.start()
    invert(fine_oct, fine_inv, 64, 0)
    invert(mid_oct, mid_inv, 8, lax.axis_index("dir") * 8)
    a_mid = theta_up(
        theta_mid[...],
        lambda r, c: c == 2 * (r % 32) + r // 32,
        lambda r, c: r == 4 * (c % 8) + c // 8,
    )
    a_top = theta_up(
        theta_top[...], lambda r, c: r == c, lambda r, c: r == 2 * (c % 32) + c // 32
    )
    b_high, b_low = block_diagonal(phi_mid[...], 4)
    b_mid = jnp.concatenate([b_high, b_high, b_low], axis=0)
    b_high, b_low = block_diagonal(phi_top[...], 2)
    b_top = jnp.concatenate([b_high, b_high, b_low], axis=0)
    loads[0].wait()
    fine_tables(angle_fine, cos_f, sin_f)
    loads[1].wait()
    for first in range(0, 8, UP_GROUP):
        chunks = []
        for octant in range(first, first + UP_GROUP):
            m = mid_inv[octant]
            for h in range(2):
                boxes = [fine_inv[m * 8 + 4 * h + b] for b in range(4)]
                for c in range(2):
                    v = [fine[box, pl.ds(c, 8, stride=2), :] for box in boxes]
                    chunks.append(jnp.concatenate(group_transpose(v), axis=0))
        w_high, w_low = split(jnp.concatenate(chunks, axis=1))
        y = dot(a_mid, jnp.concatenate([w_high, w_low, w_high], axis=0))
        y = jnp.concatenate([y[:, 128 * i : 128 * i + 128] for i in range(len(chunks))], axis=0)
        y_high, y_low = split(y)
        z = dot(jnp.concatenate([y_high, y_low, y_high], axis=1), b_mid)
        for g in range(UP_GROUP):
            real, imag = 0.0, 0.0
            for h in range(2):
                row = 256 * g + 128 * h
                for j in range(2):
                    re = z[row : row + 64, 128 * j : 128 * j + 128]
                    im = z[row + 64 : row + 128, 128 * j : 128 * j + 128]
                    cosine, sine = cos_f[2 * h + j], sin_f[2 * h + j]
                    real = real + (re * cosine - im * sine)
                    imag = imag + (re * sine + im * cosine)
            mids[first + g, 0] = real + pltpu.roll(real, 64, 1)
            mids[first + g, 1] = imag + pltpu.roll(imag, 64, 1)
    loads[2].wait()
    top_tables(angle_mid, cos_t, sin_t)
    low = lax.broadcasted_iota(jnp.int32, (64, 128), 1) < 64
    top = [0.0, 0.0]
    for first in range(0, 4, TOP_GROUP):
        chunks = [
            jnp.where(low, mids[2 * pair, c], mids[2 * pair + 1, c])
            for pair in range(first, first + TOP_GROUP)
            for c in range(2)
        ]
        w_high, w_low = split(jnp.concatenate(chunks, axis=1))
        y = dot(a_top, jnp.concatenate([w_high, w_low, w_high], axis=0))
        y = jnp.concatenate([y[:, 128 * i : 128 * i + 128] for i in range(len(chunks))], axis=0)
        y_high, y_low = split(y)
        z = dot(jnp.concatenate([y_high, y_low, y_high], axis=1), b_top)
        for g in range(TOP_GROUP):
            for j in range(2):
                re = z[256 * g : 256 * g + 128, 128 * j : 128 * j + 128]
                im = z[256 * g + 128 : 256 * g + 256, 128 * j : 128 * j + 128]
                octant = 2 * (first + g) + j
                cosine = cos_t[pl.ds(octant, 128, stride=8), :]
                sine = sin_t[pl.ds(octant, 128, stride=8), :]
                top[0] = top[0] + (re * cosine - im * sine)
                top[1] = top[1] + (re * sine + im * cosine)
    for c in range(2):
        for d in range(16):
            for x in range(2):
                out[16 * x + d, pl.ds(8 * c, 8), :] = top[c][8 * d : 8 * d + 8]


def prepare_kernel(
    angle_fine, angle_mid, theta_mid, phi_mid, theta_top, phi_top,
    cos_f, sin_f, cos_t, sin_t, a_mid, b_mid, a_top, b_top,
):
    fine_tables(angle_fine, cos_f, sin_f)
    top_tables(angle_mid, cos_t, sin_t)
    b_high, b_low = [jnp.concatenate([part, part], axis=0) for part in split(phi_top[...])]
    b_top[...] = jnp.concatenate([b_high, b_high, b_low], axis=1)
    a_top[...] = theta_down(
        theta_top[...], lambda r, c: c == 2 * (r % 32) + r // 32, lambda r, c: r == c
    )
    b_high, b_low = block_diagonal(phi_mid[...], 4)
    b_mid[...] = jnp.concatenate([b_high, b_high, b_low], axis=1)
    a_mid[...] = theta_down(
        theta_mid[...],
        lambda r, c: c == 4 * (r % 8) + r // 8,
        lambda r, c: r == 2 * (c % 32) + c // 32,
    )


def down_kernel(
    parent, fine_oct, mid_oct, cos_f, sin_f, cos_t, sin_t, a_mid, b_mid, a_top, b_top,
    out, fine_inv, mid_inv,
):
    invert(fine_oct, fine_inv, 64, 0)
    invert(mid_oct, mid_inv, 8, lax.axis_index("dir") * 8)
    field = [
        jnp.concatenate([parent[d, pl.ds(8 * c, 8), :] for d in range(16)], axis=0)
        for c in range(2)
    ]
    across = ((1,), (1,))
    for first in range(0, 8, DOWN_GROUP):
        rows = []
        for octant in range(first, first + DOWN_GROUP):
            cosine = cos_t[pl.ds(octant, 128, stride=8), :]
            sine = sin_t[pl.ds(octant, 128, stride=8), :]
            rows.append(field[0] * cosine + field[1] * sine)
            rows.append(field[1] * cosine - field[0] * sine)
        x_high, x_low = split(jnp.concatenate(rows, axis=0))
        y = dot(jnp.concatenate([x_high, x_low, x_high], axis=1), b_top[...], across)
        y = jnp.concatenate([y[128 * i : 128 * i + 128] for i in range(len(rows))], axis=1)
        y_high, y_low = split(y)
        mid = dot(a_top[...], jnp.concatenate([y_high, y_low, y_high], axis=0))
        rows = []
        for g in range(DOWN_GROUP):
            re, im = mid[:, 256 * g : 256 * g + 128], mid[:, 256 * g + 128 : 256 * g + 256]
            for h in range(2):
                c0, s0 = cos_f[2 * h], sin_f[2 * h]
                c1, s1 = cos_f[2 * h + 1], sin_f[2 * h + 1]
                rows.append(jnp.concatenate([re * c0 + im * s0, re * c1 + im * s1], axis=1))
                rows.append(jnp.concatenate([im * c0 - re * s0, im * c1 - re * s1], axis=1))
        x_high, x_low = split(jnp.concatenate(rows, axis=0))
        y = dot(jnp.concatenate([x_high, x_low, x_high], axis=1), b_mid[...], across)
        y = jnp.concatenate([y[64 * i : 64 * i + 64] for i in range(len(rows))], axis=1)
        y_high, y_low = split(y)
        w = dot(a_mid[...], jnp.concatenate([y_high, y_low, y_high], axis=0))
        for g in range(DOWN_GROUP):
            m = mid_inv[first + g]
            for h in range(2):
                boxes = [fine_inv[m * 8 + 4 * h + b] for b in range(4)]
                for c in range(2):
                    lanes = 128 * (4 * g + 2 * h + c)
                    v = group_transpose(
                        [w[8 * i : 8 * i + 8, lanes : lanes + 128] for i in range(4)]
                    )
                    for b in range(4):
                        out[boxes[b], pl.ds(c, 8, stride=2), :] = v[b]


def in_vmem(x):
    return pltpu.with_memory_space_constraint(x, pltpu.VMEM)


INVERSES = [pltpu.SMEM((64,), jnp.int32), pltpu.SMEM((8,), jnp.int32)]
TABLES = [((4, 64, 128), F32)] * 2 + [((1024, 128), F32)] * 2
DOWN_MATRICES = [((32, 192), BF16), ((128, 768), BF16), ((64, 384), BF16), ((128, 384), BF16)]


def call_up(fine, fine_oct, mid_oct, tables_of):
    return pl.pallas_call(
        up_kernel,
        out_shape=pltpu.VMEM((32, 16, 128), F32),
        in_specs=[ANY, SMEM, SMEM, ANY, ANY] + [VMEM] * 4,
        out_specs=VMEM,
        scratch_shapes=INVERSES
        + [pltpu.VMEM(*table) for table in TABLES]
        + [
            pltpu.VMEM((8, 2, 64, 128), F32),
            pltpu.VMEM((64, 16, 128), F32),
            pltpu.VMEM((256, 128), F32),
            pltpu.VMEM((1024, 128), F32),
            pltpu.SemaphoreType.DMA((3,)),
        ],
        name="upward",
    )(fine, fine_oct, mid_oct, *tables_of)


def call_prepare(tables_of):
    shapes = TABLES + DOWN_MATRICES
    return pl.pallas_call(
        prepare_kernel,
        out_shape=[pltpu.VMEM(*shape) for shape in shapes],
        in_specs=[VMEM] * 6,
        out_specs=[VMEM] * len(shapes),
        cost_estimate=pl.CostEstimate(flops=200000000, bytes_accessed=2000000, transcendentals=0),
        compiler_params=pltpu.CompilerParams(vmem_limit_bytes=12 * 2**20),
        name="prepare",
    )(*tables_of)


def call_down(parent, fine_oct, mid_oct, prepared):
    return pl.pallas_call(
        down_kernel,
        out_shape=jax.ShapeDtypeStruct((64, 16, 128), F32),
        in_specs=[VMEM, SMEM, SMEM] + [VMEM] * 8,
        out_specs=VMEM,
        scratch_shapes=INVERSES,
        compiler_params=pltpu.CompilerParams(vmem_limit_bytes=24 * 2**20),
        name="downward",
    )(in_vmem(parent), fine_oct, mid_oct, *[in_vmem(x) for x in prepared])


def add_pairs(slots, tables, fields, t, total):
    real, imag = [total[0]] + [0.0] * 3, [total[1]] + [0.0] * 3
    for k in range(32):
        fr, fi = [
            sum(field[slot[t, k], pl.ds(8 * c, 8), :] for slot, field in zip(slots, fields))
            for c in range(2)
        ]
        tr = tables[32 * t + k, pl.ds(0, 8, stride=2), :]
        ti = tables[32 * t + k, pl.ds(1, 8, stride=2), :]
        real[k % 4] = real[k % 4] + (fr * tr - fi * ti)
        imag[k % 4] = imag[k % 4] + (fr * ti + fi * tr)
    return (real[0] + real[1]) + (real[2] + real[3]), (imag[0] + imag[1]) + (imag[2] + imag[3])


def first_kernel(
    slots0, slots1, slots2, operator, fields0, fields1, fields2, tables, out, sems
):
    slots, fields = (slots0, slots1, slots2), (fields0, fields1, fields2)
    loads = [
        pltpu.make_async_copy(
            operator.at[pl.ds(32 * t, 32)], tables.at[pl.ds(32 * t, 32)], sems.at[t]
        )
        for t in range(16)
    ]
    for load in loads:
        load.start()
    for t in range(16):
        loads[t].wait()
        real, imag = add_pairs(slots, tables, fields, t, (0.0, 0.0))
        out[t, pl.ds(0, 8), :] = real
        out[t, pl.ds(8, 8), :] = imag


def last_kernel(slots, tables, fields, partial, out):
    for t in range(16):
        total = partial[t, pl.ds(0, 8), :], partial[t, pl.ds(8, 8), :]
        real, imag = add_pairs((slots,), tables, (fields,), t, total)
        out[t, pl.ds(0, 8), :] = real
        out[t, pl.ds(8, 8), :] = imag


def call_first(slots, operator, fields):
    return pl.pallas_call(
        first_kernel,
        out_shape=[pltpu.VMEM((512, 16, 128), F32), pltpu.VMEM((16, 16, 128), F32)],
        in_specs=[SMEM] * 3 + [pl.BlockSpec(memory_space=pltpu.HBM)] + [VMEM] * 3,
        out_specs=[VMEM, VMEM],
        scratch_shapes=[pltpu.SemaphoreType.DMA((16,))],
        cost_estimate=pl.CostEstimate(flops=200000000, bytes_accessed=6000000, transcendentals=0),
        compiler_params=pltpu.CompilerParams(vmem_limit_bytes=8 * 2**20),
        name="first",
    )(
        *slots,
        pltpu.with_memory_space_constraint(operator, pltpu.HBM),
        *[in_vmem(field) for field in fields],
    )


def call_last(slots, tables, fields, partial):
    return pl.pallas_call(
        last_kernel,
        out_shape=pltpu.VMEM((16, 16, 128), F32),
        in_specs=[SMEM, VMEM, VMEM, VMEM],
        out_specs=VMEM,
        compiler_params=pltpu.CompilerParams(vmem_limit_bytes=6 * 2**20),
        name="last",
    )(slots, in_vmem(tables), in_vmem(fields), in_vmem(partial))


def permutations():
    place = lambda x, y, core: x * 16 + (y % 8) * 2 + core
    every = [(x, y, core) for x in range(2) for y in range(8) for core in range(2)]
    ring = lambda by: [(place(x, y, c), place(x, y + (by, -by)[c], 1 - c)) for x, y, c in every]
    other = [(place(x, y, c), place(x, y, 1 - c)) for x, y, c in every]
    return ring(1), ring(-1), other


def gather_tops(own):
    first, second, other = permutations()
    send = lambda x, perm: lax.ppermute(x, "sub", perm)
    zero = jnp.zeros_like(own[:1])
    up, down = [], []
    a = b = own
    for _ in range(3):
        a, b = send(b, first), send(a, second)
        up.append(a)
        down.append(b)
    half = own.shape[0] // 2
    fourth_a = send(b[:half], first)
    fourth_b = send(a[half:], second)
    early = jnp.concatenate([own, up[0], up[1], down[1], down[0], zero], axis=0)
    early_far = send(early, other)
    late = jnp.concatenate([up[2], fourth_a, fourth_b, down[2], zero], axis=0)
    late_far = send(late, other)
    return early, late, early_far, late_far


def slots_of(boxes, my_sub):
    sub, slot = boxes // 16, boxes % 16
    rise = (sub // 2 - my_sub // 2) % 8
    holder = (sub + rise) % 2
    step = jnp.where(holder == 0, rise, (8 - rise) % 8)
    far = holder != my_sub % 2
    late = (step >= 3) & (step <= 5)
    place = jnp.where(step >= 3, step - 3, step) * 32 + (sub // 16) * 16 + slot
    early_slots = [jnp.where((far == side) & ~late, place, 160) for side in (False, True)]
    late_slots = [jnp.where((far == side) & late, place, 96) for side in (False, True)]
    return early_slots[0], late_slots[0], early_slots[1], late_slots[1]


def body(
    fine_fields,
    fine_octant,
    mid_octant,
    shift_fine,
    shift_mid,
    interp_theta_mid,
    interp_phi_mid,
    interp_theta_top,
    interp_phi_top,
    partners,
    translation,
):
    my_sub = lax.axis_index("sub")
    fine = fine_fields.reshape(64, 2, 8, 128).transpose(0, 2, 1, 3).reshape(64, 16, 128)
    operator = translation.reshape(512, 2, 8, 128).transpose(0, 2, 1, 3).reshape(512, 16, 128)
    tables_of = (
        shift_fine.reshape(8, 32, 128).transpose(1, 0, 2).reshape(256, 128),
        shift_mid.reshape(8, 128, 128).transpose(1, 0, 2).reshape(1024, 128),
        interp_theta_mid.T,
        interp_phi_mid.T,
        interp_theta_top.T,
        interp_phi_top.T,
    )
    slots = slots_of(partners, my_sub)
    top = call_up(fine, fine_octant, mid_octant, tables_of)
    prepared = call_prepare(tables_of)
    pairs = [
        [(x * 16 + i) * 16 + d for x in range(2) for d in range(16)] for i in range(16)
    ]
    own = lax.all_to_all(
        top, ("sub", "dir"), split_axis=0, concat_axis=0, tiled=True, axis_index_groups=pairs
    )
    fields = gather_tops(own)
    tables, partial = call_first(slots[:3], operator, fields[:3])
    incoming = call_last(slots[3], tables, fields[3], partial)
    parent = lax.all_to_all(incoming, "dir", split_axis=0, concat_axis=0, tiled=True)
    result = call_down(parent, fine_octant, mid_octant, prepared)
    return result.reshape(64, 8, 2, 128).transpose(0, 2, 1, 3).reshape(64, 2, 1024)


def solution(mesh):
    in_specs = (
        P(("sub", "dir"), None, None),
        P(("sub", "dir")),
        P("sub"),
        P(),
        P(),
        P(),
        P(),
        P(),
        P(),
        P("sub", None),
        P("sub", None, None, "dir"),
    )
    out_specs = P(("sub", "dir"), None, None)
    return jax.shard_map(body, mesh=mesh, in_specs=in_specs, out_specs=out_specs, check_vma=False)
```

profile of v0, /device:TPU:16, one launch (start us, length us, event | category | flops | bytes accessed | tf_op | source)
XLA Modules:
  0.0 98.9 jit_solution(9507901047310888793)
XLA Ops:
  0.0 4.5 %upward.1 = f32[32,16,128]{2,1,0:T(8,128)S(1)} custom-call(f32[64,16,128]{2,1,0:T(8,128)} %bitcast.42, s32[64]{0:T(128)} %fine_oct.3, s32[128]{0:T(128)} %mid_oct.3, f32[256,128]{1,0:T(8,128)} %bitcast.31, f32[1024,128]{1,0:T(8,128)} %bitcast.29, f32[32,64]{1,0:T(8,128)} %bitcast.37, f32[32,64]{1,0:T(8,128)} %bitcast.39, f32[64,128]{1,0:T(8,128)} %bitcast.33, ...), custom_call_target="tpu_custom_call" | custom-call | tf_op jit(solution)/shard_map/upward/pallas_call | solution.py:297
  4.5 25.7 %all_to_all.10 = f32[32,16,128]{2,1,0:T(8,128)S(1)} all-to-all(f32[32,16,128]{2,1,0:T(8,128)S(1)} %upward.1), channel_id=1, replica_groups={{0,1,2,3,4,5,6,7,8,9,10,11,12,13,14,15,256,257,258,259,260,261,262,263,..., dimensions={0} | all-to-all | bytes 524288 | tf_op jit(solution)/shard_map/all_to_all | solution.py:480
  30.2 1.9 %collective-permute-start.1 = (f32[32,16,128]{2,1,0:T(8,128)S(1)}, f32[32,16,128]{2,1,0:T(8,128)S(1)}, u32[]{:S(2)}, u32[]{:S(2)}) collective-permute-start(f32[32,16,128]{2,1,0:T(8,128)S(1)} %all_to_all.10), channel_id=1, source_target_pairs={{0,240},{16,32},{32,16},{48,64},{64,48},{80,96},{96,80},{112,128},... | collective-permute-start | bytes 786440 | tf_op jit(solution)/shard_map/ppermute | solution.py:419
  32.1 6.0 %collective-permute-start = (f32[32,16,128]{2,1,0:T(8,128)S(1)}, f32[32,16,128]{2,1,0:T(8,128)S(1)}, u32[]{:S(2)}, u32[]{:S(2)}) collective-permute-start(f32[32,16,128]{2,1,0:T(8,128)S(1)} %all_to_all.10), channel_id=1, source_target_pairs={{0,48},{16,224},{32,80},{48,0},{64,112},{80,32},{96,144},{112,64},... | collective-permute-start | bytes 786440 | tf_op jit(solution)/shard_map/ppermute | solution.py:419
  38.1 0.0 collective-permute-done.1
  38.1 5.1 %collective-permute-start.2 = (f32[32,16,128]{2,1,0:T(8,128)S(1)}, f32[32,16,128]{2,1,0:T(8,128)S(1)}, u32[]{:S(2)}, u32[]{:S(2)}) collective-permute-start(f32[32,16,128]{2,1,0:T(8,128)S(1)} %collective-permute-done.1), channel_id=1, source_target_pairs={{0,48},{16,224},{32,80},{48,0},{64,112},{80,32},{96,144},{112,64},... | collective-permute-start | bytes 786440 | tf_op jit(solution)/shard_map/ppermute | solution.py:419
  43.2 0.0 collective-permute-done
  43.3 1.9 %collective-permute-start.3 = (f32[32,16,128]{2,1,0:T(8,128)S(1)}, f32[32,16,128]{2,1,0:T(8,128)S(1)}, u32[]{:S(2)}, u32[]{:S(2)}) collective-permute-start(f32[32,16,128]{2,1,0:T(8,128)S(1)} %collective-permute-done), channel_id=1, source_target_pairs={{0,240},{16,32},{32,16},{48,64},{64,48},{80,96},{96,80},{112,128},... | collective-permute-start | bytes 786440 | tf_op jit(solution)/shard_map/ppermute | solution.py:419
  45.2 3.0 %collective-permute-done.2 = f32[32,16,128]{2,1,0:T(8,128)S(1)} collective-permute-done((f32[32,16,128]{2,1,0:T(8,128)S(1)}, f32[32,16,128]{2,1,0:T(8,128)S(1)}, u32[]{:S(2)}, u32[]{:S(2)}) %collective-permute-start.2) | collective-permute-done | bytes 262176 | tf_op jit(solution)/shard_map/ppermute | solution.py:419
  48.2 1.9 %collective-permute-start.5 = (f32[32,16,128]{2,1,0:T(8,128)S(1)}, f32[32,16,128]{2,1,0:T(8,128)S(1)}, u32[]{:S(2)}, u32[]{:S(2)}) collective-permute-start(f32[32,16,128]{2,1,0:T(8,128)S(1)} %collective-permute-done.2), channel_id=1, source_target_pairs={{0,240},{16,32},{32,16},{48,64},{64,48},{80,96},{96,80},{112,128},... | collective-permute-start | bytes 786440 | tf_op jit(solution)/shard_map/ppermute | solution.py:419
  50.1 0.8 collective-permute-done.3
  50.9 3.8 %collective-permute-start.4 = (f32[32,16,128]{2,1,0:T(8,128)S(1)}, f32[32,16,128]{2,1,0:T(8,128)S(1)}, u32[]{:S(2)}, u32[]{:S(2)}) collective-permute-start(f32[32,16,128]{2,1,0:T(8,128)S(1)} %collective-permute-done.3), channel_id=1, source_target_pairs={{0,48},{16,224},{32,80},{48,0},{64,112},{80,32},{96,144},{112,64},... | collective-permute-start | bytes 786440 | tf_op jit(solution)/shard_map/ppermute | solution.py:419
  54.8 0.0 copy-start.8
  54.8 1.4 %collective-permute-done.5 = f32[32,16,128]{2,1,0:T(8,128)S(1)} collective-permute-done((f32[32,16,128]{2,1,0:T(8,128)S(1)}, f32[32,16,128]{2,1,0:T(8,128)S(1)}, u32[]{:S(2)}, u32[]{:S(2)}) %collective-permute-start.5) | collective-permute-done | bytes 262176 | tf_op jit(solution)/shard_map/ppermute | solution.py:419
  56.3 6.6 %collective-permute-start.6 = (f32[16,16,128]{2,1,0:T(8,128)S(1)}, f32[16,16,128]{2,1,0:T(8,128)S(1)}, u32[]{:S(2)}, u32[]{:S(2)}) collective-permute-start(f32[16,16,128]{2,1,0:T(8,128)S(1)} %slice.8), channel_id=1, source_target_pairs={{0,48},{16,224},{32,80},{48,0},{64,112},{80,32},{96,144},{112,64},... | collective-permute-start | bytes 393224 | tf_op jit(solution)/shard_map/ppermute | solution.py:419
  62.9 1.9 %collective-permute-start.8 = (f32[161,16,128]{2,1,0:T(8,128)S(1)}, f32[161,16,128]{2,1,0:T(8,128)S(1)}, u32[]{:S(2)}, u32[]{:S(2)}) collective-permute-start(f32[161,16,128]{2,1,0:T(8,128)S(1)} %constant_dynamic-update-slice_fusion.fields0), channel_id=1, source_target_pairs={{0,16},{16,0},{32,48},{48,32},{64,80},{80,64},{96,112},{112,96},{1... | collective-permute-start | bytes 3956744 | tf_op jit(solution)/shard_map/ppermute | solution.py:419
  64.8 0.0 collective-permute-done.4
  64.8 1.9 %collective-permute-start.7 = (f32[16,16,128]{2,1,0:T(8,128)S(1)}, f32[16,16,128]{2,1,0:T(8,128)S(1)}, u32[]{:S(2)}, u32[]{:S(2)}) collective-permute-start(f32[16,16,128]{2,1,0:T(8,128)S(1)} %slice.9), channel_id=1, source_target_pairs={{0,240},{16,32},{32,16},{48,64},{64,48},{80,96},{96,80},{112,128},... | collective-permute-start | bytes 393224 | tf_op jit(solution)/shard_map/ppermute | solution.py:419
  66.8 0.0 collective-permute-done.6
  66.8 4.3 %collective-permute-done.7 = f32[16,16,128]{2,1,0:T(8,128)S(1)} collective-permute-done((f32[16,16,128]{2,1,0:T(8,128)S(1)}, f32[16,16,128]{2,1,0:T(8,128)S(1)}, u32[]{:S(2)}, u32[]{:S(2)}) %collective-permute-start.7) | collective-permute-done | bytes 131104 | tf_op jit(solution)/shard_map/ppermute | solution.py:419
  71.2 2.4 %collective-permute-start.9 = (f32[97,16,128]{2,1,0:T(8,128)S(1)}, f32[97,16,128]{2,1,0:T(8,128)}, u32[]{:S(2)}, u32[]{:S(2)}) collective-permute-start(f32[97,16,128]{2,1,0:T(8,128)S(1)} %constant_dynamic-update-slice_fusion.6.fields1), channel_id=1, source_target_pairs={{0,16},{16,0},{32,48},{48,32},{64,80},{80,64},{96,112},{112,96},{1... | collective-permute-start | bytes 2383880 | tf_op jit(solution)/shard_map/ppermute | solution.py:419
  73.6 0.0 copy-done.8
  73.7 0.0 collective-permute-done.8.fields2
  73.7 3.7 %first.1 = (f32[512,16,128]{2,1,0:T(8,128)S(1)}, f32[16,16,128]{2,1,0:T(8,128)S(1)}) custom-call(s32[16,32]{1,0:T(8,128)S(1)} %get-tuple-element.30.slots0, s32[16,32]{1,0:T(8,128)S(1)} %get-tuple-element.29.slots1, s32[16,32]{1,0:T(8,128)S(1)} %get-tuple-element.25.slots2, f32[512,16,128]{2,1,0:T(8,128)} %bitcast.41, ...), custom_call_target="tpu_custom_call" | custom-call | flops 200000000 | bytes 6000000 | tf_op jit(solution)/shard_map/first/pallas_call | solution.py:382
  77.4 0.0 collective-permute-done.9.fields
  77.4 0.0 copy-start
  77.5 0.0 copy-start.1
  77.5 0.0 copy-start.2
  77.5 0.0 copy-start.3
  77.5 0.0 copy-start.4
  77.5 0.0 copy-start.5
  77.5 0.0 copy-start.6
  77.5 0.0 copy-start.7
  77.5 2.6 %last.1 = f32[16,16,128]{2,1,0:T(8,128)} custom-call(s32[16,32]{1,0:T(8,128)S(1)} %get-tuple-element.31.slots, f32[512,16,128]{2,1,0:T(8,128)S(1)} %get-tuple-element.15.tables, f32[97,16,128]{2,1,0:T(8,128)} %collective-permute-done.9.fields, f32[16,16,128]{2,1,0:T(8,128)S(1)} %get-tuple-element.16.partial), custom_call_target="tpu_custom_call" | custom-call | tf_op jit(solution)/shard_map/last/pallas_call | solution.py:399
  80.1 3.7 %all-to-all-start.1 = ((f32[16,16,128]{2,1,0:T(8,128)}), f32[16,16,128]{2,1,0:T(8,128)S(1)}, u32[]{:S(2)}, u32[]{:S(2)}) async-start(f32[16,16,128]{2,1,0:T(8,128)} %last.1), calls=%async_computation.1 | async-start | bytes 262144 | tf_op jit(solution)/shard_map/all_to_all | solution.py:486
  83.8 0.0 copy-done
  83.8 0.0 copy-done.1
  83.8 0.0 copy-done.2
  83.9 0.0 copy-done.3
  83.9 0.0 copy-done.4
  83.9 0.0 copy-done.5
  83.9 1.0 prepare.1
  84.8 9.2 %all-to-all-done.1.parent = f32[16,16,128]{2,1,0:T(8,128)S(1)} async-done(((f32[16,16,128]{2,1,0:T(8,128)}), f32[16,16,128]{2,1,0:T(8,128)S(1)}, u32[]{:S(2)}, u32[]{:S(2)}) %all-to-all-start.1) | async-done | bytes 131104 | tf_op jit(solution)/shard_map/all_to_all | solution.py:486
  94.1 0.0 copy-done.6
  94.1 0.0 copy-done.7
  94.1 4.8 %downward.1 = f32[64,16,128]{2,1,0:T(8,128)} custom-call(f32[16,16,128]{2,1,0:T(8,128)S(1)} %all-to-all-done.1.parent, s32[64]{0:T(128)S(1)} %copy-done.6, s32[128]{0:T(128)S(1)} %copy-done.7, f32[4,64,128]{2,1,0:T(8,128)S(1)} %get-tuple-element.17.cos_f, f32[4,64,128]{2,1,0:T(8,128)S(1)} %get-tuple-element.18.sin_f, ...), custom_call_target="tpu_custom_call" | custom-call | tf_op jit(solution)/shard_map/downward/pallas_call | solution.py:329
  (15 shorter events, 0.2 us)
Async XLA Ops:
  30.2 7.9 %collective-permute-start.1 = (f32[32,16,128]{2,1,0:T(8,128)S(1)}, f32[32,16,128]{2,1,0:T(8,128)S(1)}, u32[]{:S(2)}, u32[]{:S(2)}) collective-permute-start(f32[32,16,128]{2,1,0:T(8,128)S(1)} %all_to_all.10), channel_id=1, source_target_pairs={{0,240},{16,32},{32,16},{48,64},{64,48},{80,96},{96,80},{112,128},... | collective-permute-start | bytes 786440 | tf_op jit(solution)/shard_map/ppermute | solution.py:419
  32.1 11.1 %collective-permute-start = (f32[32,16,128]{2,1,0:T(8,128)S(1)}, f32[32,16,128]{2,1,0:T(8,128)S(1)}, u32[]{:S(2)}, u32[]{:S(2)}) collective-permute-start(f32[32,16,128]{2,1,0:T(8,128)S(1)} %all_to_all.10), channel_id=1, source_target_pairs={{0,48},{16,224},{32,80},{48,0},{64,112},{80,32},{96,144},{112,64},... | collective-permute-start | bytes 786440 | tf_op jit(solution)/shard_map/ppermute | solution.py:419
  38.1 10.1 %collective-permute-start.2 = (f32[32,16,128]{2,1,0:T(8,128)S(1)}, f32[32,16,128]{2,1,0:T(8,128)S(1)}, u32[]{:S(2)}, u32[]{:S(2)}) collective-permute-start(f32[32,16,128]{2,1,0:T(8,128)S(1)} %collective-permute-done.1), channel_id=1, source_target_pairs={{0,48},{16,224},{32,80},{48,0},{64,112},{80,32},{96,144},{112,64},... | collective-permute-start | bytes 786440 | tf_op jit(solution)/shard_map/ppermute | solution.py:419
  43.3 7.7 %collective-permute-start.3 = (f32[32,16,128]{2,1,0:T(8,128)S(1)}, f32[32,16,128]{2,1,0:T(8,128)S(1)}, u32[]{:S(2)}, u32[]{:S(2)}) collective-permute-start(f32[32,16,128]{2,1,0:T(8,128)S(1)} %collective-permute-done), channel_id=1, source_target_pairs={{0,240},{16,32},{32,16},{48,64},{64,48},{80,96},{96,80},{112,128},... | collective-permute-start | bytes 786440 | tf_op jit(solution)/shard_map/ppermute | solution.py:419
  48.2 8.1 %collective-permute-start.5 = (f32[32,16,128]{2,1,0:T(8,128)S(1)}, f32[32,16,128]{2,1,0:T(8,128)S(1)}, u32[]{:S(2)}, u32[]{:S(2)}) collective-permute-start(f32[32,16,128]{2,1,0:T(8,128)S(1)} %collective-permute-done.2), channel_id=1, source_target_pairs={{0,240},{16,32},{32,16},{48,64},{64,48},{80,96},{96,80},{112,128},... | collective-permute-start | bytes 786440 | tf_op jit(solution)/shard_map/ppermute | solution.py:419
  50.9 13.9 %collective-permute-start.4 = (f32[32,16,128]{2,1,0:T(8,128)S(1)}, f32[32,16,128]{2,1,0:T(8,128)S(1)}, u32[]{:S(2)}, u32[]{:S(2)}) collective-permute-start(f32[32,16,128]{2,1,0:T(8,128)S(1)} %collective-permute-done.3), channel_id=1, source_target_pairs={{0,48},{16,224},{32,80},{48,0},{64,112},{80,32},{96,144},{112,64},... | collective-permute-start | bytes 786440 | tf_op jit(solution)/shard_map/ppermute | solution.py:419
  54.8 18.9 %copy-start.8 = (s32[16,32]{1,0:T(8,128)S(1)}, s32[16,32]{1,0:T(8,128)}, u32[]{:S(2)}) copy-start(s32[16,32]{1,0:T(8,128)} %param.20) | copy-start | bytes 6148
  56.3 10.5 %collective-permute-start.6 = (f32[16,16,128]{2,1,0:T(8,128)S(1)}, f32[16,16,128]{2,1,0:T(8,128)S(1)}, u32[]{:S(2)}, u32[]{:S(2)}) collective-permute-start(f32[16,16,128]{2,1,0:T(8,128)S(1)} %slice.8), channel_id=1, source_target_pairs={{0,48},{16,224},{32,80},{48,0},{64,112},{80,32},{96,144},{112,64},... | collective-permute-start | bytes 393224 | tf_op jit(solution)/shard_map/ppermute | solution.py:419
  62.9 10.8 %collective-permute-start.8 = (f32[161,16,128]{2,1,0:T(8,128)S(1)}, f32[161,16,128]{2,1,0:T(8,128)S(1)}, u32[]{:S(2)}, u32[]{:S(2)}) collective-permute-start(f32[161,16,128]{2,1,0:T(8,128)S(1)} %constant_dynamic-update-slice_fusion.fields0), channel_id=1, source_target_pairs={{0,16},{16,0},{32,48},{48,32},{64,80},{80,64},{96,112},{112,96},{1... | collective-permute-start | bytes 3956744 | tf_op jit(solution)/shard_map/ppermute | solution.py:419
  64.8 6.3 %collective-permute-start.7 = (f32[16,16,128]{2,1,0:T(8,128)S(1)}, f32[16,16,128]{2,1,0:T(8,128)S(1)}, u32[]{:S(2)}, u32[]{:S(2)}) collective-permute-start(f32[16,16,128]{2,1,0:T(8,128)S(1)} %slice.9), channel_id=1, source_target_pairs={{0,240},{16,32},{32,16},{48,64},{64,48},{80,96},{96,80},{112,128},... | collective-permute-start | bytes 393224 | tf_op jit(solution)/shard_map/ppermute | solution.py:419
  71.2 6.2 %collective-permute-start.9 = (f32[97,16,128]{2,1,0:T(8,128)S(1)}, f32[97,16,128]{2,1,0:T(8,128)}, u32[]{:S(2)}, u32[]{:S(2)}) collective-permute-start(f32[97,16,128]{2,1,0:T(8,128)S(1)} %constant_dynamic-update-slice_fusion.6.fields1), channel_id=1, source_target_pairs={{0,16},{16,0},{32,48},{48,32},{64,80},{80,64},{96,112},{112,96},{1... | collective-permute-start | bytes 2383880 | tf_op jit(solution)/shard_map/ppermute | solution.py:419
  77.4 6.4 %copy-start = (f32[8,16384]{1,0:T(8,128)S(1)}, f32[8,16384]{1,0:T(8,128)}, u32[]{:S(2)}) copy-start(f32[8,16384]{1,0:T(8,128)} %param.15) | copy-start | bytes 1572868
  77.5 6.4 %copy-start.1 = (f32[8,4096]{1,0:T(8,128)S(1)}, f32[8,4096]{1,0:T(8,128)}, u32[]{:S(2)}) copy-start(f32[8,4096]{1,0:T(8,128)} %param.14) | copy-start | bytes 393220
  77.5 6.4 %copy-start.2 = (f32[128,64]{0,1:T(8,128)S(1)}, f32[128,64]{0,1:T(8,128)}, u32[]{:S(2)}) copy-start(f32[128,64]{0,1:T(8,128)} %param.18) | copy-start | bytes 98308
  77.5 6.4 %copy-start.3 = (f32[128,64]{0,1:T(8,128)S(1)}, f32[128,64]{0,1:T(8,128)}, u32[]{:S(2)}) copy-start(f32[128,64]{0,1:T(8,128)} %param.19) | copy-start | bytes 98308
  77.5 6.4 %copy-start.4 = (f32[64,32]{0,1:T(8,128)S(1)}, f32[64,32]{0,1:T(8,128)}, u32[]{:S(2)}) copy-start(f32[64,32]{0,1:T(8,128)} %param.16) | copy-start | bytes 24580
  77.5 6.4 %copy-start.5 = (f32[64,32]{0,1:T(8,128)S(1)}, f32[64,32]{0,1:T(8,128)}, u32[]{:S(2)}) copy-start(f32[64,32]{0,1:T(8,128)} %param.17) | copy-start | bytes 24580
  77.5 16.6 %copy-start.6 = (s32[64]{0:T(128)S(1)}, s32[64]{0:T(128)}, u32[]{:S(2)}) copy-start(s32[64]{0:T(128)} %fine_oct.3) | copy-start | bytes 772
  77.5 16.6 %copy-start.7 = (s32[128]{0:T(128)S(1)}, s32[128]{0:T(128)}, u32[]{:S(2)}) copy-start(s32[128]{0:T(128)} %mid_oct.3) | copy-start | bytes 1540
  80.1 14.0 %all-to-all-start.1 = ((f32[16,16,128]{2,1,0:T(8,128)}), f32[16,16,128]{2,1,0:T(8,128)S(1)}, u32[]{:S(2)}, u32[]{:S(2)}) async-start(f32[16,16,128]{2,1,0:T(8,128)} %last.1), calls=%async_computation.1 | async-start | bytes 262144 | tf_op jit(solution)/shard_map/all_to_all | solution.py:486
where the time goes:
time: 99.5 us; the launch traced here: 98.9 us
  starting transfers between devices  37.1 us (37%)
  blocking collectives  25.7 us (26%)
  waiting for transfers between devices  18.8 us (19%)
  Pallas kernels  16.6 us (17%)
    ppermute x10, starting transfers between devices, gather_tops(): send = lambda x, perm: lax.ppermute(x, 'sub', perm)  33.5 us
    all_to_all x1, blocking collectives, body(): lax.all_to_all(top, ('sub', 'dir'), split_axis=0, concat_axis=0, tiled=Tr...  25.7 us
    ppermute x10, waiting for transfers between devices, gather_tops(): send = lambda x, perm: lax.ppermute(x, 'sub', perm)  9.52 us
    all_to_all x1, waiting for transfers between devices, body(): lax.all_to_all(incoming, 'dir', split_axis=0, concat_axis=0, tiled=True)  9.25 us
    pallas_call x1, Pallas kernels, call_down(): pl.pallas_call(down_kernel, out_shape=jax.ShapeDtypeStruct((64, 16, 128),...  4.85 us
    pallas_call x1, Pallas kernels, call_up(): pl.pallas_call(up_kernel, out_shape=pltpu.VMEM((32, 16, 128), F32), in_sp...  4.53 us
    pallas_call x1, Pallas kernels, call_first(): pl.pallas_call(first_kernel, out_shape=[pltpu.VMEM((512, 16, 128), F32),...  3.71 us
    all_to_all x1, starting transfers between devices, body(): lax.all_to_all(incoming, 'dir', split_axis=0, concat_axis=0, tiled=True)  3.68 us
  transfers between devices with their start and end apart: 11, of which 5 were waited for; matrix products, arithmetic and copies ran while one was open for 0% of the time, Pallas kernels for 5%

commit v1 on v0

--- a/solution.py
+++ b/solution.py
@@ -128,22 +128,18 @@
     return (dot(high, first) + dot(low, last)).astype(BF16)
 
 
-def up_kernel(
-    fine_hbm, fine_oct, mid_oct, angle_fine_hbm, angle_mid_hbm,
-    theta_mid, phi_mid, theta_top, phi_top,
-    out, fine_inv, mid_inv, cos_f, sin_f, cos_t, sin_t, mids,
-    fine, angle_fine, angle_mid, sems,
-):
+def up_kernel(*refs):
+    sources, (out, fine_inv, mid_inv, cos_f, sin_f, cos_t, sin_t, mids) = refs[:9], refs[9:17]
+    targets, sems = refs[17:26], refs[26]
     loads = [
         pltpu.make_async_copy(source, target, sems.at[i])
-        for i, (source, target) in enumerate(
-            ((angle_fine_hbm, angle_fine), (fine_hbm, fine), (angle_mid_hbm, angle_mid))
-        )
-    ]
-    for load in loads:
-        load.start()
-    invert(fine_oct, fine_inv, 64, 0)
-    invert(mid_oct, mid_inv, 8, lax.axis_index("dir") * 8)
+        for i, (source, target) in enumerate(zip(sources, targets))
+    ]
+    fine, fine_oct, mid_oct, angle_fine, angle_mid, theta_mid, phi_mid, theta_top, phi_top = targets
+    for i in (5, 6, 7, 8, 3, 1, 2, 0, 4):
+        loads[i].start()
+    for i in (5, 6, 7, 8):
+        loads[i].wait()
     a_mid = theta_up(
         theta_mid[...],
         lambda r, c: c == 2 * (r % 32) + r // 32,
@@ -156,9 +152,13 @@
     b_mid = jnp.concatenate([b_high, b_high, b_low], axis=0)
     b_high, b_low = block_diagonal(phi_top[...], 2)
     b_top = jnp.concatenate([b_high, b_high, b_low], axis=0)
-    loads[0].wait()
+    loads[3].wait()
     fine_tables(angle_fine, cos_f, sin_f)
     loads[1].wait()
+    loads[2].wait()
+    invert(fine_oct, fine_inv, 64, 0)
+    invert(mid_oct, mid_inv, 8, lax.axis_index("dir") * 8)
+    loads[0].wait()
     for first in range(0, 8, UP_GROUP):
         chunks = []
         for octant in range(first, first + UP_GROUP):
@@ -185,7 +185,7 @@
                     imag = imag + (re * sine + im * cosine)
             mids[first + g, 0] = real + pltpu.roll(real, 64, 1)
             mids[first + g, 1] = imag + pltpu.roll(imag, 64, 1)
-    loads[2].wait()
+    loads[4].wait()
     top_tables(angle_mid, cos_t, sin_t)
     low = lax.broadcasted_iota(jnp.int32, (64, 128), 1) < 64
     top = [0.0, 0.0]
@@ -237,8 +237,9 @@
 
 def down_kernel(
     parent, fine_oct, mid_oct, cos_f, sin_f, cos_t, sin_t, a_mid, b_mid, a_top, b_top,
-    out, fine_inv, mid_inv,
+    out_hbm, fine_inv, mid_inv, out, sems,
 ):
+    stores = []
     invert(fine_oct, fine_inv, 64, 0)
     invert(mid_oct, mid_inv, 8, lax.axis_index("dir") * 8)
     field = [
@@ -282,6 +283,13 @@
                     )
                     for b in range(4):
                         out[boxes[b], pl.ds(c, 8, stride=2), :] = v[b]
+            group = pl.ds(m * 8, 8)
+            stores.append(
+                pltpu.make_async_copy(out.at[group], out_hbm.at[group], sems.at[first + g])
+            )
+            stores[-1].start()
+    for store in stores:
+        store.wait()
 
 
 def in_vmem(x):
@@ -297,16 +305,22 @@
     return pl.pallas_call(
         up_kernel,
         out_shape=pltpu.VMEM((32, 16, 128), F32),
-        in_specs=[ANY, SMEM, SMEM, ANY, ANY] + [VMEM] * 4,
+        in_specs=[ANY] * 9,
         out_specs=VMEM,
         scratch_shapes=INVERSES
         + [pltpu.VMEM(*table) for table in TABLES]
         + [
             pltpu.VMEM((8, 2, 64, 128), F32),
             pltpu.VMEM((64, 16, 128), F32),
+            pltpu.SMEM((64,), jnp.int32),
+            pltpu.SMEM((128,), jnp.int32),
             pltpu.VMEM((256, 128), F32),
             pltpu.VMEM((1024, 128), F32),
-            pltpu.SemaphoreType.DMA((3,)),
+            pltpu.VMEM((32, 64), F32),
+            pltpu.VMEM((32, 64), F32),
+            pltpu.VMEM((64, 128), F32),
+            pltpu.VMEM((64, 128), F32),
+            pltpu.SemaphoreType.DMA((9,)),
         ],
         name="upward",
     )(fine, fine_oct, mid_oct, *tables_of)
@@ -330,8 +344,9 @@
         down_kernel,
         out_shape=jax.ShapeDtypeStruct((64, 16, 128), F32),
         in_specs=[VMEM, SMEM, SMEM] + [VMEM] * 8,
-        out_specs=VMEM,
-        scratch_shapes=INVERSES,
+        out_specs=ANY,
+        scratch_shapes=INVERSES
+        + [pltpu.VMEM((64, 16, 128), F32), pltpu.SemaphoreType.DMA((8,))],
         compiler_params=pltpu.CompilerParams(vmem_limit_bytes=24 * 2**20),
         name="downward",
     )(in_vmem(parent), fine_oct, mid_oct, *[in_vmem(x) for x in prepared])
@@ -352,20 +367,27 @@
 
 
 def first_kernel(
-    slots0, slots1, slots2, operator, fields0, fields1, fields2, tables, out, sems
+    slots0, slots1, slots2, operator, fields0, fields1, fields2,
+    tables, out, listed0, listed1, listed2, sems, slot_sems,
 ):
-    slots, fields = (slots0, slots1, slots2), (fields0, fields1, fields2)
+    listed, fields = (listed0, listed1, listed2), (fields0, fields1, fields2)
+    lists = [
+        pltpu.make_async_copy(source, target, slot_sems.at[i])
+        for i, (source, target) in enumerate(zip((slots0, slots1, slots2), listed))
+    ]
     loads = [
         pltpu.make_async_copy(
             operator.at[pl.ds(32 * t, 32)], tables.at[pl.ds(32 * t, 32)], sems.at[t]
         )
         for t in range(16)
     ]
-    for load in loads:
-        load.start()
+    for copy in lists + loads:
+        copy.start()
+    for copy in lists:
+        copy.wait()
     for t in range(16):
         loads[t].wait()
-        real, imag = add_pairs(slots, tables, fields, t, (0.0, 0.0))
+        real, imag = add_pairs(listed, tables, fields, t, (0.0, 0.0))
         out[t, pl.ds(0, 8), :] = real
         out[t, pl.ds(8, 8), :] = imag
 
@@ -382,9 +404,10 @@
     return pl.pallas_call(
         first_kernel,
         out_shape=[pltpu.VMEM((512, 16, 128), F32), pltpu.VMEM((16, 16, 128), F32)],
-        in_specs=[SMEM] * 3 + [pl.BlockSpec(memory_space=pltpu.HBM)] + [VMEM] * 3,
+        in_specs=[ANY] * 3 + [pl.BlockSpec(memory_space=pltpu.HBM)] + [VMEM] * 3,
         out_specs=[VMEM, VMEM],
-        scratch_shapes=[pltpu.SemaphoreType.DMA((16,))],
+        scratch_shapes=[pltpu.SMEM((16, 32), jnp.int32)] * 3
+        + [pltpu.SemaphoreType.DMA((16,)), pltpu.SemaphoreType.DMA((3,))],
         cost_estimate=pl.CostEstimate(flops=200000000, bytes_accessed=6000000, transcendentals=0),
         compiler_params=pltpu.CompilerParams(vmem_limit_bytes=8 * 2**20),
         name="first",

time: 99.5 us -> 98.4 us (0.989)
  Pallas kernels: 16.6 us -> 15.6 us
  transfers between devices with their start and end apart: 11 -> 11, of which waited for: 5 -> 5; matrix products, arithmetic and copies ran while one was open for 0% -> 0% of each run, Pallas kernels for 5% -> 4%
where the time goes in v1:
time: 98.4 us; the launch traced here: 97.9 us
  starting transfers between devices  37.1 us (38%)
  blocking collectives  25.7 us (26%)
  waiting for transfers between devices  18.7 us (19%)
  Pallas kernels  15.6 us (16%)
    ppermute x10, starting transfers between devices, gather_tops(): send = lambda x, perm: lax.ppermute(x, 'sub', perm)  33.5 us
    all_to_all x1, blocking collectives, body(): lax.all_to_all(top, ('sub', 'dir'), split_axis=0, concat_axis=0, tiled=Tr...  25.7 us
    ppermute x10, waiting for transfers between devices, gather_tops(): send = lambda x, perm: lax.ppermute(x, 'sub', perm)  9.5 us
    all_to_all x1, waiting for transfers between devices, body(): lax.all_to_all(incoming, 'dir', split_axis=0, concat_axis=0, tiled=True)  9.25 us
    pallas_call x1, Pallas kernels, call_down(): pl.pallas_call(down_kernel, out_shape=jax.ShapeDtypeStruct((64, 16, 128),...  4.75 us
    pallas_call x1, Pallas kernels, call_up(): pl.pallas_call(up_kernel, out_shape=pltpu.VMEM((32, 16, 128), F32), in_sp...  4.54 us
    all_to_all x1, starting transfers between devices, body(): lax.all_to_all(incoming, 'dir', split_axis=0, concat_axis=0, tiled=True)  3.68 us
    pallas_call x1, Pallas kernels, call_first(): pl.pallas_call(first_kernel, out_shape=[pltpu.VMEM((512, 16, 128), F32),...  2.75 us
  transfers between devices with their start and end apart: 11, of which 5 were waited for; matrix products, arithmetic and copies ran while one was open for 0% of the time, Pallas kernels for 4%

profile of v1, /device:TPU:16, one launch (start us, length us, event | category | flops | bytes accessed | tf_op | source)
XLA Modules:
  0.0 97.9 jit_solution(8586007264436041619)
XLA Ops:
  0.0 4.5 %upward.1 = f32[32,16,128]{2,1,0:T(8,128)S(1)} custom-call(f32[64,16,128]{2,1,0:T(8,128)} %bitcast.42, s32[64]{0:T(128)} %fine_oct.1, s32[128]{0:T(128)} %mid_oct.1, f32[256,128]{1,0:T(8,128)} %bitcast.31, f32[1024,128]{1,0:T(8,128)} %bitcast.29, f32[32,64]{1,0:T(8,128)} %bitcast.37, f32[32,64]{1,0:T(8,128)} %bitcast.39, f32[64,128]{1,0:T(8,128)} %bitcast.33, ...), custom_call_target="tpu_custom_call" | custom-call | tf_op jit(solution)/shard_map/upward/pallas_call | solution.py:305
  4.5 25.7 %all_to_all.10 = f32[32,16,128]{2,1,0:T(8,128)S(1)} all-to-all(f32[32,16,128]{2,1,0:T(8,128)S(1)} %upward.1), channel_id=1, replica_groups={{0,1,2,3,4,5,6,7,8,9,10,11,12,13,14,15,256,257,258,259,260,261,262,263,..., dimensions={0} | all-to-all | bytes 524288 | tf_op jit(solution)/shard_map/all_to_all | solution.py:503
  30.2 1.9 %collective-permute-start.1 = (f32[32,16,128]{2,1,0:T(8,128)S(1)}, f32[32,16,128]{2,1,0:T(8,128)S(1)}, u32[]{:S(2)}, u32[]{:S(2)}) collective-permute-start(f32[32,16,128]{2,1,0:T(8,128)S(1)} %all_to_all.10), channel_id=1, source_target_pairs={{0,240},{16,32},{32,16},{48,64},{64,48},{80,96},{96,80},{112,128},... | collective-permute-start | bytes 786440 | tf_op jit(solution)/shard_map/ppermute | solution.py:442
  32.1 6.0 %collective-permute-start = (f32[32,16,128]{2,1,0:T(8,128)S(1)}, f32[32,16,128]{2,1,0:T(8,128)S(1)}, u32[]{:S(2)}, u32[]{:S(2)}) collective-permute-start(f32[32,16,128]{2,1,0:T(8,128)S(1)} %all_to_all.10), channel_id=1, source_target_pairs={{0,48},{16,224},{32,80},{48,0},{64,112},{80,32},{96,144},{112,64},... | collective-permute-start | bytes 786440 | tf_op jit(solution)/shard_map/ppermute | solution.py:442
  38.1 0.0 collective-permute-done.1
  38.1 5.1 %collective-permute-start.2 = (f32[32,16,128]{2,1,0:T(8,128)S(1)}, f32[32,16,128]{2,1,0:T(8,128)S(1)}, u32[]{:S(2)}, u32[]{:S(2)}) collective-permute-start(f32[32,16,128]{2,1,0:T(8,128)S(1)} %collective-permute-done.1), channel_id=1, source_target_pairs={{0,48},{16,224},{32,80},{48,0},{64,112},{80,32},{96,144},{112,64},... | collective-permute-start | bytes 786440 | tf_op jit(solution)/shard_map/ppermute | solution.py:442
  43.2 0.0 collective-permute-done
  43.3 1.9 %collective-permute-start.3 = (f32[32,16,128]{2,1,0:T(8,128)S(1)}, f32[32,16,128]{2,1,0:T(8,128)S(1)}, u32[]{:S(2)}, u32[]{:S(2)}) collective-permute-start(f32[32,16,128]{2,1,0:T(8,128)S(1)} %collective-permute-done), channel_id=1, source_target_pairs={{0,240},{16,32},{32,16},{48,64},{64,48},{80,96},{96,80},{112,128},... | collective-permute-start | bytes 786440 | tf_op jit(solution)/shard_map/ppermute | solution.py:442
  45.2 3.0 %collective-permute-done.2 = f32[32,16,128]{2,1,0:T(8,128)S(1)} collective-permute-done((f32[32,16,128]{2,1,0:T(8,128)S(1)}, f32[32,16,128]{2,1,0:T(8,128)S(1)}, u32[]{:S(2)}, u32[]{:S(2)}) %collective-permute-start.2) | collective-permute-done | bytes 262176 | tf_op jit(solution)/shard_map/ppermute | solution.py:442
  48.2 1.9 %collective-permute-start.5 = (f32[32,16,128]{2,1,0:T(8,128)S(1)}, f32[32,16,128]{2,1,0:T(8,128)S(1)}, u32[]{:S(2)}, u32[]{:S(2)}) collective-permute-start(f32[32,16,128]{2,1,0:T(8,128)S(1)} %collective-permute-done.2), channel_id=1, source_target_pairs={{0,240},{16,32},{32,16},{48,64},{64,48},{80,96},{96,80},{112,128},... | collective-permute-start | bytes 786440 | tf_op jit(solution)/shard_map/ppermute | solution.py:442
  50.1 0.8 collective-permute-done.3
  50.9 3.8 %collective-permute-start.4 = (f32[32,16,128]{2,1,0:T(8,128)S(1)}, f32[32,16,128]{2,1,0:T(8,128)S(1)}, u32[]{:S(2)}, u32[]{:S(2)}) collective-permute-start(f32[32,16,128]{2,1,0:T(8,128)S(1)} %collective-permute-done.3), channel_id=1, source_target_pairs={{0,48},{16,224},{32,80},{48,0},{64,112},{80,32},{96,144},{112,64},... | collective-permute-start | bytes 786440 | tf_op jit(solution)/shard_map/ppermute | solution.py:442
  54.8 0.0 copy-start.8
  54.8 1.4 %collective-permute-done.5 = f32[32,16,128]{2,1,0:T(8,128)S(1)} collective-permute-done((f32[32,16,128]{2,1,0:T(8,128)S(1)}, f32[32,16,128]{2,1,0:T(8,128)S(1)}, u32[]{:S(2)}, u32[]{:S(2)}) %collective-permute-start.5) | collective-permute-done | bytes 262176 | tf_op jit(solution)/shard_map/ppermute | solution.py:442
  56.2 6.6 %collective-permute-start.6 = (f32[16,16,128]{2,1,0:T(8,128)S(1)}, f32[16,16,128]{2,1,0:T(8,128)S(1)}, u32[]{:S(2)}, u32[]{:S(2)}) collective-permute-start(f32[16,16,128]{2,1,0:T(8,128)S(1)} %slice.8), channel_id=1, source_target_pairs={{0,48},{16,224},{32,80},{48,0},{64,112},{80,32},{96,144},{112,64},... | collective-permute-start | bytes 393224 | tf_op jit(solution)/shard_map/ppermute | solution.py:442
  62.9 1.9 %collective-permute-start.8 = (f32[161,16,128]{2,1,0:T(8,128)S(1)}, f32[161,16,128]{2,1,0:T(8,128)S(1)}, u32[]{:S(2)}, u32[]{:S(2)}) collective-permute-start(f32[161,16,128]{2,1,0:T(8,128)S(1)} %constant_dynamic-update-slice_fusion.fields0), channel_id=1, source_target_pairs={{0,16},{16,0},{32,48},{48,32},{64,80},{80,64},{96,112},{112,96},{1... | collective-permute-start | bytes 3956744 | tf_op jit(solution)/shard_map/ppermute | solution.py:442
  64.8 0.0 collective-permute-done.4
  64.8 1.9 %collective-permute-start.7 = (f32[16,16,128]{2,1,0:T(8,128)S(1)}, f32[16,16,128]{2,1,0:T(8,128)S(1)}, u32[]{:S(2)}, u32[]{:S(2)}) collective-permute-start(f32[16,16,128]{2,1,0:T(8,128)S(1)} %slice.9), channel_id=1, source_target_pairs={{0,240},{16,32},{32,16},{48,64},{64,48},{80,96},{96,80},{112,128},... | collective-permute-start | bytes 393224 | tf_op jit(solution)/shard_map/ppermute | solution.py:442
  66.8 0.0 collective-permute-done.6
  66.8 4.3 %collective-permute-done.7 = f32[16,16,128]{2,1,0:T(8,128)S(1)} collective-permute-done((f32[16,16,128]{2,1,0:T(8,128)S(1)}, f32[16,16,128]{2,1,0:T(8,128)S(1)}, u32[]{:S(2)}, u32[]{:S(2)}) %collective-permute-start.7) | collective-permute-done | bytes 131104 | tf_op jit(solution)/shard_map/ppermute | solution.py:442
  71.2 2.4 %collective-permute-start.9 = (f32[97,16,128]{2,1,0:T(8,128)S(1)}, f32[97,16,128]{2,1,0:T(8,128)}, u32[]{:S(2)}, u32[]{:S(2)}) collective-permute-start(f32[97,16,128]{2,1,0:T(8,128)S(1)} %constant_dynamic-update-slice_fusion.6.fields1), channel_id=1, source_target_pairs={{0,16},{16,0},{32,48},{48,32},{64,80},{80,64},{96,112},{112,96},{1... | collective-permute-start | bytes 2383880 | tf_op jit(solution)/shard_map/ppermute | solution.py:442
  73.6 0.0 copy-done.8
  73.7 0.0 collective-permute-done.8.fields2
  73.7 2.8 %first.1 = (f32[512,16,128]{2,1,0:T(8,128)S(1)}, f32[16,16,128]{2,1,0:T(8,128)S(1)}) custom-call(s32[16,32]{1,0:T(8,128)S(1)} %get-tuple-element.30.slots0, s32[16,32]{1,0:T(8,128)S(1)} %get-tuple-element.29.slots1, s32[16,32]{1,0:T(8,128)S(1)} %get-tuple-element.25.slots2, f32[512,16,128]{2,1,0:T(8,128)} %bitcast.41, ...), custom_call_target="tpu_custom_call" | custom-call | flops 200000000 | bytes 6000000 | tf_op jit(solution)/shard_map/first/pallas_call | solution.py:404
  76.5 0.0 collective-permute-done.9.fields
  76.5 0.0 copy-start
  76.5 0.0 copy-start.1
  76.5 0.0 copy-start.2
  76.5 0.0 copy-start.3
  76.5 0.0 copy-start.4
  76.5 0.0 copy-start.5
  76.5 0.0 copy-start.6
  76.5 0.0 copy-start.7
  76.6 2.6 %last.1 = f32[16,16,128]{2,1,0:T(8,128)} custom-call(s32[16,32]{1,0:T(8,128)S(1)} %get-tuple-element.31.slots, f32[512,16,128]{2,1,0:T(8,128)S(1)} %get-tuple-element.15.tables, f32[97,16,128]{2,1,0:T(8,128)} %collective-permute-done.9.fields, f32[16,16,128]{2,1,0:T(8,128)S(1)} %get-tuple-element.16.partial), custom_call_target="tpu_custom_call" | custom-call | tf_op jit(solution)/shard_map/last/pallas_call | solution.py:422
  79.2 3.7 %all-to-all-start.1 = ((f32[16,16,128]{2,1,0:T(8,128)}), f32[16,16,128]{2,1,0:T(8,128)S(1)}, u32[]{:S(2)}, u32[]{:S(2)}) async-start(f32[16,16,128]{2,1,0:T(8,128)} %last.1), calls=%async_computation.1 | async-start | bytes 262144 | tf_op jit(solution)/shard_map/all_to_all | solution.py:509
  82.8 0.0 copy-done
  82.9 0.0 copy-done.1
  82.9 0.0 copy-done.2
  82.9 0.0 copy-done.3
  82.9 0.0 copy-done.4
  82.9 0.0 copy-done.5
  82.9 1.0 prepare.1
  83.9 9.2 %all-to-all-done.1.parent = f32[16,16,128]{2,1,0:T(8,128)S(1)} async-done(((f32[16,16,128]{2,1,0:T(8,128)}), f32[16,16,128]{2,1,0:T(8,128)S(1)}, u32[]{:S(2)}, u32[]{:S(2)}) %all-to-all-start.1) | async-done | bytes 131104 | tf_op jit(solution)/shard_map/all_to_all | solution.py:509
  93.1 0.0 copy-done.6
  93.1 0.0 copy-done.7
  93.1 4.8 %downward.1 = f32[64,16,128]{2,1,0:T(8,128)} custom-call(f32[16,16,128]{2,1,0:T(8,128)S(1)} %all-to-all-done.1.parent, s32[64]{0:T(128)S(1)} %copy-done.6, s32[128]{0:T(128)S(1)} %copy-done.7, f32[4,64,128]{2,1,0:T(8,128)S(1)} %get-tuple-element.17.cos_f, f32[4,64,128]{2,1,0:T(8,128)S(1)} %get-tuple-element.18.sin_f, ...), custom_call_target="tpu_custom_call" | custom-call | tf_op jit(solution)/shard_map/downward/pallas_call | solution.py:343
  (15 shorter events, 0.2 us)
Async XLA Ops:
  30.2 7.9 %collective-permute-start.1 = (f32[32,16,128]{2,1,0:T(8,128)S(1)}, f32[32,16,128]{2,1,0:T(8,128)S(1)}, u32[]{:S(2)}, u32[]{:S(2)}) collective-permute-start(f32[32,16,128]{2,1,0:T(8,128)S(1)} %all_to_all.10), channel_id=1, source_target_pairs={{0,240},{16,32},{32,16},{48,64},{64,48},{80,96},{96,80},{112,128},... | collective-permute-start | bytes 786440 | tf_op jit(solution)/shard_map/ppermute | solution.py:442
  32.1 11.1 %collective-permute-start = (f32[32,16,128]{2,1,0:T(8,128)S(1)}, f32[32,16,128]{2,1,0:T(8,128)S(1)}, u32[]{:S(2)}, u32[]{:S(2)}) collective-permute-start(f32[32,16,128]{2,1,0:T(8,128)S(1)} %all_to_all.10), channel_id=1, source_target_pairs={{0,48},{16,224},{32,80},{48,0},{64,112},{80,32},{96,144},{112,64},... | collective-permute-start | bytes 786440 | tf_op jit(solution)/shard_map/ppermute | solution.py:442
  38.1 10.0 %collective-permute-start.2 = (f32[32,16,128]{2,1,0:T(8,128)S(1)}, f32[32,16,128]{2,1,0:T(8,128)S(1)}, u32[]{:S(2)}, u32[]{:S(2)}) collective-permute-start(f32[32,16,128]{2,1,0:T(8,128)S(1)} %collective-permute-done.1), channel_id=1, source_target_pairs={{0,48},{16,224},{32,80},{48,0},{64,112},{80,32},{96,144},{112,64},... | collective-permute-start | bytes 786440 | tf_op jit(solution)/shard_map/ppermute | solution.py:442
  43.3 7.7 %collective-permute-start.3 = (f32[32,16,128]{2,1,0:T(8,128)S(1)}, f32[32,16,128]{2,1,0:T(8,128)S(1)}, u32[]{:S(2)}, u32[]{:S(2)}) collective-permute-start(f32[32,16,128]{2,1,0:T(8,128)S(1)} %collective-permute-done), channel_id=1, source_target_pairs={{0,240},{16,32},{32,16},{48,64},{64,48},{80,96},{96,80},{112,128},... | collective-permute-start | bytes 786440 | tf_op jit(solution)/shard_map/ppermute | solution.py:442
  48.2 8.0 %collective-permute-start.5 = (f32[32,16,128]{2,1,0:T(8,128)S(1)}, f32[32,16,128]{2,1,0:T(8,128)S(1)}, u32[]{:S(2)}, u32[]{:S(2)}) collective-permute-start(f32[32,16,128]{2,1,0:T(8,128)S(1)} %collective-permute-done.2), channel_id=1, source_target_pairs={{0,240},{16,32},{32,16},{48,64},{64,48},{80,96},{96,80},{112,128},... | collective-permute-start | bytes 786440 | tf_op jit(solution)/shard_map/ppermute | solution.py:442
  50.9 13.9 %collective-permute-start.4 = (f32[32,16,128]{2,1,0:T(8,128)S(1)}, f32[32,16,128]{2,1,0:T(8,128)S(1)}, u32[]{:S(2)}, u32[]{:S(2)}) collective-permute-start(f32[32,16,128]{2,1,0:T(8,128)S(1)} %collective-permute-done.3), channel_id=1, source_target_pairs={{0,48},{16,224},{32,80},{48,0},{64,112},{80,32},{96,144},{112,64},... | collective-permute-start | bytes 786440 | tf_op jit(solution)/shard_map/ppermute | solution.py:442
  54.8 18.8 %copy-start.8 = (s32[16,32]{1,0:T(8,128)S(1)}, s32[16,32]{1,0:T(8,128)}, u32[]{:S(2)}) copy-start(s32[16,32]{1,0:T(8,128)} %param.20) | copy-start | bytes 6148
  56.2 10.6 %collective-permute-start.6 = (f32[16,16,128]{2,1,0:T(8,128)S(1)}, f32[16,16,128]{2,1,0:T(8,128)S(1)}, u32[]{:S(2)}, u32[]{:S(2)}) collective-permute-start(f32[16,16,128]{2,1,0:T(8,128)S(1)} %slice.8), channel_id=1, source_target_pairs={{0,48},{16,224},{32,80},{48,0},{64,112},{80,32},{96,144},{112,64},... | collective-permute-start | bytes 393224 | tf_op jit(solution)/shard_map/ppermute | solution.py:442
  62.9 10.8 %collective-permute-start.8 = (f32[161,16,128]{2,1,0:T(8,128)S(1)}, f32[161,16,128]{2,1,0:T(8,128)S(1)}, u32[]{:S(2)}, u32[]{:S(2)}) collective-permute-start(f32[161,16,128]{2,1,0:T(8,128)S(1)} %constant_dynamic-update-slice_fusion.fields0), channel_id=1, source_target_pairs={{0,16},{16,0},{32,48},{48,32},{64,80},{80,64},{96,112},{112,96},{1... | collective-permute-start | bytes 3956744 | tf_op jit(solution)/shard_map/ppermute | solution.py:442
  64.8 6.3 %collective-permute-start.7 = (f32[16,16,128]{2,1,0:T(8,128)S(1)}, f32[16,16,128]{2,1,0:T(8,128)S(1)}, u32[]{:S(2)}, u32[]{:S(2)}) collective-permute-start(f32[16,16,128]{2,1,0:T(8,128)S(1)} %slice.9), channel_id=1, source_target_pairs={{0,240},{16,32},{32,16},{48,64},{64,48},{80,96},{96,80},{112,128},... | collective-permute-start | bytes 393224 | tf_op jit(solution)/shard_map/ppermute | solution.py:442
  71.2 5.3 %collective-permute-start.9 = (f32[97,16,128]{2,1,0:T(8,128)S(1)}, f32[97,16,128]{2,1,0:T(8,128)}, u32[]{:S(2)}, u32[]{:S(2)}) collective-permute-start(f32[97,16,128]{2,1,0:T(8,128)S(1)} %constant_dynamic-update-slice_fusion.6.fields1), channel_id=1, source_target_pairs={{0,16},{16,0},{32,48},{48,32},{64,80},{80,64},{96,112},{112,96},{1... | collective-permute-start | bytes 2383880 | tf_op jit(solution)/shard_map/ppermute | solution.py:442
  76.5 6.4 %copy-start = (f32[8,16384]{1,0:T(8,128)S(1)}, f32[8,16384]{1,0:T(8,128)}, u32[]{:S(2)}) copy-start(f32[8,16384]{1,0:T(8,128)} %param.15) | copy-start | bytes 1572868
  76.5 6.4 %copy-start.1 = (f32[8,4096]{1,0:T(8,128)S(1)}, f32[8,4096]{1,0:T(8,128)}, u32[]{:S(2)}) copy-start(f32[8,4096]{1,0:T(8,128)} %param.14) | copy-start | bytes 393220
  76.5 6.4 %copy-start.2 = (f32[128,64]{0,1:T(8,128)S(1)}, f32[128,64]{0,1:T(8,128)}, u32[]{:S(2)}) copy-start(f32[128,64]{0,1:T(8,128)} %param.18) | copy-start | bytes 98308
  76.5 6.4 %copy-start.3 = (f32[128,64]{0,1:T(8,128)S(1)}, f32[128,64]{0,1:T(8,128)}, u32[]{:S(2)}) copy-start(f32[128,64]{0,1:T(8,128)} %param.19) | copy-start | bytes 98308
  76.5 6.4 %copy-start.4 = (f32[64,32]{0,1:T(8,128)S(1)}, f32[64,32]{0,1:T(8,128)}, u32[]{:S(2)}) copy-start(f32[64,32]{0,1:T(8,128)} %param.16) | copy-start | bytes 24580
  76.5 6.4 %copy-start.5 = (f32[64,32]{0,1:T(8,128)S(1)}, f32[64,32]{0,1:T(8,128)}, u32[]{:S(2)}) copy-start(f32[64,32]{0,1:T(8,128)} %param.17) | copy-start | bytes 24580
  76.5 16.6 %copy-start.6 = (s32[64]{0:T(128)S(1)}, s32[64]{0:T(128)}, u32[]{:S(2)}) copy-start(s32[64]{0:T(128)} %fine_oct.1) | copy-start | bytes 772
  76.5 16.6 %copy-start.7 = (s32[128]{0:T(128)S(1)}, s32[128]{0:T(128)}, u32[]{:S(2)}) copy-start(s32[128]{0:T(128)} %mid_oct.1) | copy-start | bytes 1540
  79.2 14.0 %all-to-all-start.1 = ((f32[16,16,128]{2,1,0:T(8,128)}), f32[16,16,128]{2,1,0:T(8,128)S(1)}, u32[]{:S(2)}, u32[]{:S(2)}) async-start(f32[16,16,128]{2,1,0:T(8,128)} %last.1), calls=%async_computation.1 | async-start | bytes 262144 | tf_op jit(solution)/shard_map/all_to_all | solution.py:509

commit v2 on v1

--- a/solution.py
+++ b/solution.py
@@ -447,12 +447,10 @@
         a, b = send(b, first), send(a, second)
         up.append(a)
         down.append(b)
-    half = own.shape[0] // 2
-    fourth_a = send(b[:half], first)
-    fourth_b = send(a[half:], second)
+    fourth = send(b, first)
     early = jnp.concatenate([own, up[0], up[1], down[1], down[0], zero], axis=0)
     early_far = send(early, other)
-    late = jnp.concatenate([up[2], fourth_a, fourth_b, down[2], zero], axis=0)
+    late = jnp.concatenate([up[2], fourth, down[2], zero], axis=0)
     late_far = send(late, other)
     return early, late, early_far, late_far
 

time: 98.4 us -> 93.7 us (0.952)
  the two profiles are of different devices: /device:TPU:16 before, /device:TPU:24 now
where the time goes in v2:
time: 93.7 us; the launch traced here: 93.2 us
  starting transfers between devices  29.7 us (32%)
  blocking collectives  25.7 us (27%)
  waiting for transfers between devices  21.6 us (23%)
  Pallas kernels  15.6 us (17%)
    ppermute x9, starting transfers between devices, gather_tops(): send = lambda x, perm: lax.ppermute(x, 'sub', perm)  26 us
    all_to_all x1, blocking collectives, body(): lax.all_to_all(top, ('sub', 'dir'), split_axis=0, concat_axis=0, tiled=Tr...  25.7 us
    ppermute x9, waiting for transfers between devices, gather_tops(): send = lambda x, perm: lax.ppermute(x, 'sub', perm)  12.4 us
    all_to_all x1, waiting for transfers between devices, body(): lax.all_to_all(incoming, 'dir', split_axis=0, concat_axis=0, tiled=True)  9.2 us
    pallas_call x1, Pallas kernels, call_down(): pl.pallas_call(down_kernel, out_shape=jax.ShapeDtypeStruct((64, 16, 128),...  4.75 us
    pallas_call x1, Pallas kernels, call_up(): pl.pallas_call(up_kernel, out_shape=pltpu.VMEM((32, 16, 128), F32), in_sp...  4.55 us
    all_to_all x1, starting transfers between devices, body(): lax.all_to_all(incoming, 'dir', split_axis=0, concat_axis=0, tiled=True)  3.68 us
    pallas_call x1, Pallas kernels, call_first(): pl.pallas_call(first_kernel, out_shape=[pltpu.VMEM((512, 16, 128), F32),...  2.75 us
  transfers between devices with their start and end apart: 10, of which 7 were waited for; matrix products, arithmetic and copies ran while one was open for 0% of the time, Pallas kernels for 4%

profile of v2, /device:TPU:24, one launch (start us, length us, event | category | flops | bytes accessed | tf_op | source)
XLA Modules:
  0.0 93.2 jit_solution(6840301977665322769)
XLA Ops:
  0.0 4.5 %upward.1 = f32[32,16,128]{2,1,0:T(8,128)S(1)} custom-call(f32[64,16,128]{2,1,0:T(8,128)} %bitcast.42, s32[64]{0:T(128)} %fine_oct.1, s32[128]{0:T(128)} %mid_oct.1, f32[256,128]{1,0:T(8,128)} %bitcast.31, f32[1024,128]{1,0:T(8,128)} %bitcast.29, f32[32,64]{1,0:T(8,128)} %bitcast.37, f32[32,64]{1,0:T(8,128)} %bitcast.39, f32[64,128]{1,0:T(8,128)} %bitcast.33, ...), custom_call_target="tpu_custom_call" | custom-call | tf_op jit(solution)/shard_map/upward/pallas_call | solution.py:305
  4.6 25.7 %all_to_all.10 = f32[32,16,128]{2,1,0:T(8,128)S(1)} all-to-all(f32[32,16,128]{2,1,0:T(8,128)S(1)} %upward.1), channel_id=1, replica_groups={{0,1,2,3,4,5,6,7,8,9,10,11,12,13,14,15,256,257,258,259,260,261,262,263,..., dimensions={0} | all-to-all | bytes 524288 | tf_op jit(solution)/shard_map/all_to_all | solution.py:501
  30.2 1.9 %collective-permute-start.1 = (f32[32,16,128]{2,1,0:T(8,128)S(1)}, f32[32,16,128]{2,1,0:T(8,128)S(1)}, u32[]{:S(2)}, u32[]{:S(2)}) collective-permute-start(f32[32,16,128]{2,1,0:T(8,128)S(1)} %all_to_all.10), channel_id=1, source_target_pairs={{0,240},{16,32},{32,16},{48,64},{64,48},{80,96},{96,80},{112,128},... | collective-permute-start | bytes 786440 | tf_op jit(solution)/shard_map/ppermute | solution.py:442
  32.2 5.1 %collective-permute-start = (f32[32,16,128]{2,1,0:T(8,128)S(1)}, f32[32,16,128]{2,1,0:T(8,128)S(1)}, u32[]{:S(2)}, u32[]{:S(2)}) collective-permute-start(f32[32,16,128]{2,1,0:T(8,128)S(1)} %all_to_all.10), channel_id=1, source_target_pairs={{0,48},{16,224},{32,80},{48,0},{64,112},{80,32},{96,144},{112,64},... | collective-permute-start | bytes 786440 | tf_op jit(solution)/shard_map/ppermute | solution.py:442
  37.2 0.7 collective-permute-done.1
  37.9 3.8 %collective-permute-start.2 = (f32[32,16,128]{2,1,0:T(8,128)S(1)}, f32[32,16,128]{2,1,0:T(8,128)S(1)}, u32[]{:S(2)}, u32[]{:S(2)}) collective-permute-start(f32[32,16,128]{2,1,0:T(8,128)S(1)} %collective-permute-done.1), channel_id=1, source_target_pairs={{0,48},{16,224},{32,80},{48,0},{64,112},{80,32},{96,144},{112,64},... | collective-permute-start | bytes 786440 | tf_op jit(solution)/shard_map/ppermute | solution.py:442
  41.7 0.4 collective-permute-done
  42.1 1.9 %collective-permute-start.3 = (f32[32,16,128]{2,1,0:T(8,128)S(1)}, f32[32,16,128]{2,1,0:T(8,128)S(1)}, u32[]{:S(2)}, u32[]{:S(2)}) collective-permute-start(f32[32,16,128]{2,1,0:T(8,128)S(1)} %collective-permute-done), channel_id=1, source_target_pairs={{0,240},{16,32},{32,16},{48,64},{64,48},{80,96},{96,80},{112,128},... | collective-permute-start | bytes 786440 | tf_op jit(solution)/shard_map/ppermute | solution.py:442
  44.0 2.8 %collective-permute-done.2 = f32[32,16,128]{2,1,0:T(8,128)S(1)} collective-permute-done((f32[32,16,128]{2,1,0:T(8,128)S(1)}, f32[32,16,128]{2,1,0:T(8,128)S(1)}, u32[]{:S(2)}, u32[]{:S(2)}) %collective-permute-start.2) | collective-permute-done | bytes 262176 | tf_op jit(solution)/shard_map/ppermute | solution.py:442
  46.8 1.9 %collective-permute-start.5 = (f32[32,16,128]{2,1,0:T(8,128)S(1)}, f32[32,16,128]{2,1,0:T(8,128)S(1)}, u32[]{:S(2)}, u32[]{:S(2)}) collective-permute-start(f32[32,16,128]{2,1,0:T(8,128)S(1)} %collective-permute-done.2), channel_id=1, source_target_pairs={{0,240},{16,32},{32,16},{48,64},{64,48},{80,96},{96,80},{112,128},... | collective-permute-start | bytes 786440 | tf_op jit(solution)/shard_map/ppermute | solution.py:442
  48.7 0.0 copy-start.8
  48.8 2.1 %collective-permute-done.3 = f32[32,16,128]{2,1,0:T(8,128)S(1)} collective-permute-done((f32[32,16,128]{2,1,0:T(8,128)S(1)}, f32[32,16,128]{2,1,0:T(8,128)S(1)}, u32[]{:S(2)}, u32[]{:S(2)}) %collective-permute-start.3) | collective-permute-done | bytes 262176 | tf_op jit(solution)/shard_map/ppermute | solution.py:442
  50.9 2.7 %collective-permute-start.7 = (f32[161,16,128]{2,1,0:T(8,128)S(1)}, f32[161,16,128]{2,1,0:T(8,128)S(1)}, u32[]{:S(2)}, u32[]{:S(2)}) collective-permute-start(f32[161,16,128]{2,1,0:T(8,128)S(1)} %constant_dynamic-update-slice_fusion.fields0), channel_id=1, source_target_pairs={{0,16},{16,0},{32,48},{48,32},{64,80},{80,64},{96,112},{112,96},{1... | collective-permute-start | bytes 3956744 | tf_op jit(solution)/shard_map/ppermute | solution.py:442
  53.6 4.4 %collective-permute-start.4 = (f32[32,16,128]{2,1,0:T(8,128)S(1)}, f32[32,16,128]{2,1,0:T(8,128)S(1)}, u32[]{:S(2)}, u32[]{:S(2)}) collective-permute-start(f32[32,16,128]{2,1,0:T(8,128)S(1)} %collective-permute-done.3), channel_id=1, source_target_pairs={{0,48},{16,224},{32,80},{48,0},{64,112},{80,32},{96,144},{112,64},... | collective-permute-start | bytes 786440 | tf_op jit(solution)/shard_map/ppermute | solution.py:442
  58.0 0.0 collective-permute-done.5
  58.0 2.4 %collective-permute-start.6 = (f32[32,16,128]{2,1,0:T(8,128)S(1)}, f32[32,16,128]{2,1,0:T(8,128)S(1)}, u32[]{:S(2)}, u32[]{:S(2)}) collective-permute-start(f32[32,16,128]{2,1,0:T(8,128)S(1)} %collective-permute-done.5), channel_id=1, source_target_pairs={{0,48},{16,224},{32,80},{48,0},{64,112},{80,32},{96,144},{112,64},... | collective-permute-start | bytes 786440 | tf_op jit(solution)/shard_map/ppermute | solution.py:442
  60.4 2.1 %collective-permute-done.4 = f32[32,16,128]{2,1,0:T(8,128)S(1)} collective-permute-done((f32[32,16,128]{2,1,0:T(8,128)S(1)}, f32[32,16,128]{2,1,0:T(8,128)S(1)}, u32[]{:S(2)}, u32[]{:S(2)}) %collective-permute-start.4) | collective-permute-done | bytes 262176 | tf_op jit(solution)/shard_map/ppermute | solution.py:442
  62.5 4.4 %collective-permute-done.6 = f32[32,16,128]{2,1,0:T(8,128)S(1)} collective-permute-done((f32[32,16,128]{2,1,0:T(8,128)S(1)}, f32[32,16,128]{2,1,0:T(8,128)S(1)}, u32[]{:S(2)}, u32[]{:S(2)}) %collective-permute-start.6) | collective-permute-done | bytes 262176 | tf_op jit(solution)/shard_map/ppermute | solution.py:442
  66.9 0.1 pad_maximum_fusion.fields1
  67.0 1.9 %collective-permute-start.8 = (f32[97,16,128]{2,1,0:T(8,128)S(1)}, f32[97,16,128]{2,1,0:T(8,128)}, u32[]{:S(2)}, u32[]{:S(2)}) collective-permute-start(f32[97,16,128]{2,1,0:T(8,128)S(1)} %pad_maximum_fusion.fields1), channel_id=1, source_target_pairs={{0,16},{16,0},{32,48},{48,32},{64,80},{80,64},{96,112},{112,96},{1... | collective-permute-start | bytes 2383880 | tf_op jit(solution)/shard_map/ppermute | solution.py:442
  68.9 0.0 copy-done.8
  69.0 0.0 collective-permute-done.7.fields2
  69.0 2.8 %first.1 = (f32[512,16,128]{2,1,0:T(8,128)S(1)}, f32[16,16,128]{2,1,0:T(8,128)S(1)}) custom-call(s32[16,32]{1,0:T(8,128)S(1)} %get-tuple-element.30.slots0, s32[16,32]{1,0:T(8,128)S(1)} %get-tuple-element.29.slots1, s32[16,32]{1,0:T(8,128)S(1)} %get-tuple-element.25.slots2, f32[512,16,128]{2,1,0:T(8,128)} %bitcast.41, ...), custom_call_target="tpu_custom_call" | custom-call | flops 200000000 | bytes 6000000 | tf_op jit(solution)/shard_map/first/pallas_call | solution.py:404
  71.8 0.0 collective-permute-done.8.fields
  71.8 0.0 copy-start
  71.8 0.0 copy-start.1
  71.8 0.0 copy-start.2
  71.8 0.0 copy-start.3
  71.8 0.0 copy-start.4
  71.9 0.0 copy-start.5
  71.9 0.0 copy-start.6
  71.9 0.0 copy-start.7
  71.9 2.6 %last.1 = f32[16,16,128]{2,1,0:T(8,128)} custom-call(s32[16,32]{1,0:T(8,128)S(1)} %get-tuple-element.31.slots, f32[512,16,128]{2,1,0:T(8,128)S(1)} %get-tuple-element.15.tables, f32[97,16,128]{2,1,0:T(8,128)} %collective-permute-done.8.fields, f32[16,16,128]{2,1,0:T(8,128)S(1)} %get-tuple-element.16.partial), custom_call_target="tpu_custom_call" | custom-call | tf_op jit(solution)/shard_map/last/pallas_call | solution.py:422
  74.5 3.7 %all-to-all-start.1 = ((f32[16,16,128]{2,1,0:T(8,128)}), f32[16,16,128]{2,1,0:T(8,128)S(1)}, u32[]{:S(2)}, u32[]{:S(2)}) async-start(f32[16,16,128]{2,1,0:T(8,128)} %last.1), calls=%async_computation.1 | async-start | bytes 262144 | tf_op jit(solution)/shard_map/all_to_all | solution.py:507
  78.2 0.0 copy-done
  78.2 0.0 copy-done.1
  78.2 0.0 copy-done.2
  78.2 0.0 copy-done.3
  78.2 0.0 copy-done.4
  78.2 0.0 copy-done.5
  78.2 1.0 %prepare.1 = (f32[4,64,128]{2,1,0:T(8,128)S(1)}, f32[4,64,128]{2,1,0:T(8,128)S(1)}, f32[1024,128]{1,0:T(8,128)S(1)}, f32[1024,128]{1,0:T(8,128)S(1)}, bf16[32,19...) custom-call(f32[256,128]{1,0:T(8,128)S(1)} %bitcast.32, ...), custom_call_target="tpu_custom_call" | custom-call | flops 200000000 | bytes 2000000 | tf_op jit(solution)/shard_map/prepare/pallas_call | solution.py:331
  79.2 9.2 %all-to-all-done.1.parent = f32[16,16,128]{2,1,0:T(8,128)S(1)} async-done(((f32[16,16,128]{2,1,0:T(8,128)}), f32[16,16,128]{2,1,0:T(8,128)S(1)}, u32[]{:S(2)}, u32[]{:S(2)}) %all-to-all-start.1) | async-done | bytes 131104 | tf_op jit(solution)/shard_map/all_to_all | solution.py:507
  88.4 0.0 copy-done.6
  88.4 0.0 copy-done.7
  88.4 4.8 %downward.1 = f32[64,16,128]{2,1,0:T(8,128)} custom-call(f32[16,16,128]{2,1,0:T(8,128)S(1)} %all-to-all-done.1.parent, s32[64]{0:T(128)S(1)} %copy-done.6, s32[128]{0:T(128)S(1)} %copy-done.7, f32[4,64,128]{2,1,0:T(8,128)S(1)} %get-tuple-element.17.cos_f, f32[4,64,128]{2,1,0:T(8,128)S(1)} %get-tuple-element.18.sin_f, ...), custom_call_target="tpu_custom_call" | custom-call | tf_op jit(solution)/shard_map/downward/pallas_call | solution.py:343
  (9 shorter events, 0.2 us)
Async XLA Ops:
  30.2 7.7 %collective-permute-start.1 = (f32[32,16,128]{2,1,0:T(8,128)S(1)}, f32[32,16,128]{2,1,0:T(8,128)S(1)}, u32[]{:S(2)}, u32[]{:S(2)}) collective-permute-start(f32[32,16,128]{2,1,0:T(8,128)S(1)} %all_to_all.10), channel_id=1, source_target_pairs={{0,240},{16,32},{32,16},{48,64},{64,48},{80,96},{96,80},{112,128},... | collective-permute-start | bytes 786440 | tf_op jit(solution)/shard_map/ppermute | solution.py:442
  32.2 9.9 %collective-permute-start = (f32[32,16,128]{2,1,0:T(8,128)S(1)}, f32[32,16,128]{2,1,0:T(8,128)S(1)}, u32[]{:S(2)}, u32[]{:S(2)}) collective-permute-start(f32[32,16,128]{2,1,0:T(8,128)S(1)} %all_to_all.10), channel_id=1, source_target_pairs={{0,48},{16,224},{32,80},{48,0},{64,112},{80,32},{96,144},{112,64},... | collective-permute-start | bytes 786440 | tf_op jit(solution)/shard_map/ppermute | solution.py:442
  37.9 8.9 %collective-permute-start.2 = (f32[32,16,128]{2,1,0:T(8,128)S(1)}, f32[32,16,128]{2,1,0:T(8,128)S(1)}, u32[]{:S(2)}, u32[]{:S(2)}) collective-permute-start(f32[32,16,128]{2,1,0:T(8,128)S(1)} %collective-permute-done.1), channel_id=1, source_target_pairs={{0,48},{16,224},{32,80},{48,0},{64,112},{80,32},{96,144},{112,64},... | collective-permute-start | bytes 786440 | tf_op jit(solution)/shard_map/ppermute | solution.py:442
  42.1 8.8 %collective-permute-start.3 = (f32[32,16,128]{2,1,0:T(8,128)S(1)}, f32[32,16,128]{2,1,0:T(8,128)S(1)}, u32[]{:S(2)}, u32[]{:S(2)}) collective-permute-start(f32[32,16,128]{2,1,0:T(8,128)S(1)} %collective-permute-done), channel_id=1, source_target_pairs={{0,240},{16,32},{32,16},{48,64},{64,48},{80,96},{96,80},{112,128},... | collective-permute-start | bytes 786440 | tf_op jit(solution)/shard_map/ppermute | solution.py:442
  46.8 11.2 %collective-permute-start.5 = (f32[32,16,128]{2,1,0:T(8,128)S(1)}, f32[32,16,128]{2,1,0:T(8,128)S(1)}, u32[]{:S(2)}, u32[]{:S(2)}) collective-permute-start(f32[32,16,128]{2,1,0:T(8,128)S(1)} %collective-permute-done.2), channel_id=1, source_target_pairs={{0,240},{16,32},{32,16},{48,64},{64,48},{80,96},{96,80},{112,128},... | collective-permute-start | bytes 786440 | tf_op jit(solution)/shard_map/ppermute | solution.py:442
  48.7 20.2 %copy-start.8 = (s32[16,32]{1,0:T(8,128)S(1)}, s32[16,32]{1,0:T(8,128)}, u32[]{:S(2)}) copy-start(s32[16,32]{1,0:T(8,128)} %param.20) | copy-start | bytes 6148
  50.9 18.1 %collective-permute-start.7 = (f32[161,16,128]{2,1,0:T(8,128)S(1)}, f32[161,16,128]{2,1,0:T(8,128)S(1)}, u32[]{:S(2)}, u32[]{:S(2)}) collective-permute-start(f32[161,16,128]{2,1,0:T(8,128)S(1)} %constant_dynamic-update-slice_fusion.fields0), channel_id=1, source_target_pairs={{0,16},{16,0},{32,48},{48,32},{64,80},{80,64},{96,112},{112,96},{1... | collective-permute-start | bytes 3956744 | tf_op jit(solution)/shard_map/ppermute | solution.py:442
  53.6 8.9 %collective-permute-start.4 = (f32[32,16,128]{2,1,0:T(8,128)S(1)}, f32[32,16,128]{2,1,0:T(8,128)S(1)}, u32[]{:S(2)}, u32[]{:S(2)}) collective-permute-start(f32[32,16,128]{2,1,0:T(8,128)S(1)} %collective-permute-done.3), channel_id=1, source_target_pairs={{0,48},{16,224},{32,80},{48,0},{64,112},{80,32},{96,144},{112,64},... | collective-permute-start | bytes 786440 | tf_op jit(solution)/shard_map/ppermute | solution.py:442
  58.0 8.9 %collective-permute-start.6 = (f32[32,16,128]{2,1,0:T(8,128)S(1)}, f32[32,16,128]{2,1,0:T(8,128)S(1)}, u32[]{:S(2)}, u32[]{:S(2)}) collective-permute-start(f32[32,16,128]{2,1,0:T(8,128)S(1)} %collective-permute-done.5), channel_id=1, source_target_pairs={{0,48},{16,224},{32,80},{48,0},{64,112},{80,32},{96,144},{112,64},... | collective-permute-start | bytes 786440 | tf_op jit(solution)/shard_map/ppermute | solution.py:442
  67.0 4.8 %collective-permute-start.8 = (f32[97,16,128]{2,1,0:T(8,128)S(1)}, f32[97,16,128]{2,1,0:T(8,128)}, u32[]{:S(2)}, u32[]{:S(2)}) collective-permute-start(f32[97,16,128]{2,1,0:T(8,128)S(1)} %pad_maximum_fusion.fields1), channel_id=1, source_target_pairs={{0,16},{16,0},{32,48},{48,32},{64,80},{80,64},{96,112},{112,96},{1... | collective-permute-start | bytes 2383880 | tf_op jit(solution)/shard_map/ppermute | solution.py:442
  71.8 6.4 %copy-start = (f32[8,16384]{1,0:T(8,128)S(1)}, f32[8,16384]{1,0:T(8,128)}, u32[]{:S(2)}) copy-start(f32[8,16384]{1,0:T(8,128)} %param.15) | copy-start | bytes 1572868
  71.8 6.4 %copy-start.1 = (f32[8,4096]{1,0:T(8,128)S(1)}, f32[8,4096]{1,0:T(8,128)}, u32[]{:S(2)}) copy-start(f32[8,4096]{1,0:T(8,128)} %param.14) | copy-start | bytes 393220
  71.8 6.4 %copy-start.2 = (f32[128,64]{0,1:T(8,128)S(1)}, f32[128,64]{0,1:T(8,128)}, u32[]{:S(2)}) copy-start(f32[128,64]{0,1:T(8,128)} %param.18) | copy-start | bytes 98308
  71.8 6.4 %copy-start.3 = (f32[128,64]{0,1:T(8,128)S(1)}, f32[128,64]{0,1:T(8,128)}, u32[]{:S(2)}) copy-start(f32[128,64]{0,1:T(8,128)} %param.19) | copy-start | bytes 98308
  71.8 6.4 %copy-start.4 = (f32[64,32]{0,1:T(8,128)S(1)}, f32[64,32]{0,1:T(8,128)}, u32[]{:S(2)}) copy-start(f32[64,32]{0,1:T(8,128)} %param.16) | copy-start | bytes 24580
  71.9 6.4 %copy-start.5 = (f32[64,32]{0,1:T(8,128)S(1)}, f32[64,32]{0,1:T(8,128)}, u32[]{:S(2)}) copy-start(f32[64,32]{0,1:T(8,128)} %param.17) | copy-start | bytes 24580
  71.9 16.5 %copy-start.6 = (s32[64]{0:T(128)S(1)}, s32[64]{0:T(128)}, u32[]{:S(2)}) copy-start(s32[64]{0:T(128)} %fine_oct.1) | copy-start | bytes 772
  71.9 16.5 %copy-start.7 = (s32[128]{0:T(128)S(1)}, s32[128]{0:T(128)}, u32[]{:S(2)}) copy-start(s32[128]{0:T(128)} %mid_oct.1) | copy-start | bytes 1540
  74.5 13.9 %all-to-all-start.1 = ((f32[16,16,128]{2,1,0:T(8,128)}), f32[16,16,128]{2,1,0:T(8,128)S(1)}, u32[]{:S(2)}, u32[]{:S(2)}) async-start(f32[16,16,128]{2,1,0:T(8,128)} %last.1), calls=%async_computation.1 | async-start | bytes 262144 | tf_op jit(solution)/shard_map/all_to_all | solution.py:507
